TPU v7x, 32 devices: a whole 2x2x4 slice. The times are simulated.
32 devices in a mesh: srow: 4 (over y, core), scol: 8 (over z, x).
Axes of the slice: x: 2, y: 2, z: 4, core: 2. Of those that a mesh axis runs over, the one named last changes fastest.
Arguments:
- loads: float32 [4, 16, 4, 128], P('srow', 'scol'), may hold values from -6 to 6
- local_inverse: float32 [4, 16, 128, 128], P('srow', 'scol'), as said below
- dirichlet: float32 [4, 16, 128, 128], P('srow', 'scol'), as said below
- corner_coupling: float32 [4, 16, 128], P('srow', 'scol'), may hold values from -4 to 4
- coarse_inverse: float32 [4, 16, 16], P('srow', 'scol'), as said below
- partner: int32 [4, 16, 128], P('srow', 'scol'), may hold values from -1 to 31, as said below
Outputs:
- multipliers: float32 [4, 16, 4, 128], P('srow', 'scol')
- residual: float32 [4, 16, 4, 128], P('srow', 'scol')
Inputs may be any that keep to these rules, and one draw needn't show every extreme that they name: `partner`: on each edge of each subdomain the first n entries, for some n of 1 to 32, are the positions 0 to n - 1 in order or reversed, the rest are -1; the two subdomains sharing an edge have the same n and mutually inverse lists. `local_inverse`: each block is symmetric positive definite. `dirichlet`: each block is symmetric positive definite. `coarse_inverse`: each band's matrix is symmetric positive definite.
All inputs are finite; a program needn't handle non-finite values.
Results may differ from a plain program's by a relative error of at most 0.0003.
Values sent between devices are 32-bit elements; how exact they have to be, the bound alone decides.
A program may use at most 64 MiB of HBM per device.

v0:
```python
import jax
import jax.numpy as jnp
from jax import lax
from jax.sharding import PartitionSpec as P

ITERS = 3
precise = lax.Precision.HIGHEST


def with_halo(cells, sides, width):
    for axis, dim in sides:
        count = lax.axis_size(axis)
        head = lax.slice_in_dim(cells, 0, width, axis=dim)
        tail = lax.slice_in_dim(cells, cells.shape[dim] - width, cells.shape[dim], axis=dim)
        cells = jnp.concatenate(
            [
                lax.ppermute(tail, axis, [(i, (i + 1) % count) for i in range(count)]),
                cells,
                lax.ppermute(head, axis, [((i + 1) % count, i) for i in range(count)]),
            ],
            axis=dim,
        )
    return cells


def facing_edges(values):
    edge_len = values.shape[-1] // 4
    sideways = with_halo(values[..., 0 : 2 * edge_len], (("scol", 1),), 1)
    vertical = with_halo(values[..., 2 * edge_len :], (("srow", 0),), 1)
    west_side = sideways[:, :-2, :, edge_len : 2 * edge_len]
    east_side = sideways[:, 2:, :, 0:edge_len]
    south_side = vertical[:-2, :, :, edge_len : 2 * edge_len]
    north_side = vertical[2:, :, :, 0:edge_len]
    return jnp.concatenate([west_side, east_side, south_side, north_side], axis=-1)


def jump(values, partner):
    edge_len = values.shape[-1] // 4
    facing = facing_edges(values)
    offset = jnp.arange(values.shape[-1], dtype=jnp.int32) // edge_len * edge_len
    position = jnp.clip(partner, 0, edge_len - 1) + offset
    position = jnp.broadcast_to(position[:, :, None, :], values.shape)
    picked = jnp.take_along_axis(facing, position, axis=-1)
    return jnp.where(partner[:, :, None, :] >= 0, values - picked, jnp.zeros_like(values))


def apply_inverse(values, local_inverse, corner_coupling, coarse_inverse):
    sub_rows, sub_cols, rhs_count, width = values.shape
    blocks = jnp.einsum("ijab,ijrb->ijra", local_inverse, values, precision=precise)
    coarse_in = jnp.einsum("ijb,ijrb->ijr", corner_coupling, values, precision=precise)
    coarse_in = coarse_in.reshape(sub_rows * sub_cols, rhs_count)
    band_rows = coarse_inverse[0]
    coarse_out = jnp.dot(
        band_rows,
        lax.all_gather(coarse_in, "scol", axis=0, tiled=True),
        precision=precise,
        preferred_element_type=jnp.float32,
    )
    coarse_out = coarse_out.reshape(sub_rows, sub_cols, rhs_count)
    return blocks + corner_coupling[:, :, None, :] * coarse_out[..., None]


def inner(left, right):
    return jnp.sum(left * right, axis=(0, 1, 3))


def global_sums(first_dot, second_dot):
    return lax.psum((first_dot, second_dot), ("srow", "scol"))


def scaled(coef, values):
    return coef[None, None, :, None] * values


def body(loads, local_inverse, dirichlet, corner_coupling, coarse_inverse, partner):

    def operator(values):
        spread = jump(values, partner)
        return jump(apply_inverse(spread, local_inverse, corner_coupling, coarse_inverse), partner)

    def precond(values):
        spread = jump(values, partner)
        return jump(jnp.einsum("ijab,ijrb->ijra", dirichlet, spread, precision=precise), partner)

    right = operator(loads)
    multipliers = jnp.zeros_like(right)
    residual = right
    precon = precond(residual)
    image = operator(precon)
    gamma, curvature = global_sums(inner(residual, precon), inner(precon, image))
    step_size = gamma / curvature
    search = precon
    along = image
    for iteration in range(ITERS):
        multipliers = multipliers + scaled(step_size, search)
        residual = residual - scaled(step_size, along)
        if iteration + 1 < ITERS:
            precon = precond(residual)
            image = operator(precon)
            gamma_new, curvature = global_sums(inner(residual, precon), inner(precon, image))
            dir_ratio = gamma_new / gamma
            step_size = gamma_new / (curvature - dir_ratio * gamma_new / step_size)
            search = precon + scaled(dir_ratio, search)
            along = image + scaled(dir_ratio, along)
            gamma = gamma_new
    return (multipliers, residual)


def solution(mesh):
    return jax.shard_map(
        body,
        mesh=mesh,
        in_specs=(
            P("srow", "scol", None, None),
            P("srow", "scol", None, None),
            P("srow", "scol", None, None),
            P("srow", "scol", None),
            P("srow", "scol", None),
            P("srow", "scol", None),
        ),
        out_specs=(P("srow", "scol", None, None), P("srow", "scol", None, None)),
        check_vma=False,
    )
```

profile of v0, /device:TPU:0, one launch (start us, length us, event | category | flops | bytes accessed | tf_op | source)
XLA Modules:
  0.0 464.1 jit_solution(16173901481340105120)
XLA Ops:
  2.0 1.9 collective-permute-start.3
  4.0 2.3 collective-permute-start
  6.2 3.1 collective-permute-start.1
  10.9 9.6 %gather_fusion = f32[1024]{0:T(1024)S(1)} fusion(f32[2,4,128]{2,1,0:T(4,128)S(1)} %fusion.69, s32[1024]{0:T(1024)S(1)} %bitcast.196), kind=kCustom, calls=%fused_computation.clone | custom fusion | bytes 20480 | tf_op jit(solution)/shard_map/jit(take_along_axis)/gather | solution.py:43
  21.3 21.1 %all-gather = f32[8,2,4]{2,1,0:T(2,128)S(1)} all-gather(f32[1,2,4]{2,1,0:T(2,128)S(1)} %bitcast.256), channel_id=1, replica_groups=mesh['srow'=4,'scol'=8] {'scol'}, dimensions={0}, use_global_device_ids=true | all-gather | bytes 288 | tf_op jit(solution)/shard_map/all_gather | solution.py:55
  43.6 1.7 collective-permute-start.7
  45.4 4.7 %collective-permute-start.5 = (f32[1,1,4,64]{3,2,1,0:T(4,128)S(1)}, f32[1,1,4,64]{3,2,1,0:T(4,128)S(1)}, u32[]{:S(2)}, u32[]{:S(2)}) collective-permute-start(f32[1,1,4,64]{3,2,1,0:T(4,128)S(1)} %get-tuple-element.76), channel_id=1, source_target_pairs={{1,0},{2,1},{3,2},{4,3},{5,4},{6,5},{7,6},{0,7},{9,8},{10,9},{11,1... | collective-permute-start | bytes 3080 | tf_op jit(solution)/shard_map/ppermute | solution.py:19
  50.2 1.5 collective-permute-done.4
  51.7 9.6 %gather_fusion.1 = f32[1024]{0:T(1024)S(1)} fusion(f32[2,4,128]{2,1,0:T(4,128)S(1)} %fusion.65, s32[1024]{0:T(1024)S(1)} %bitcast.197), kind=kCustom, calls=%fused_computation.1.clone | custom fusion | bytes 20480 | tf_op jit(solution)/shard_map/jit(take_along_axis)/gather | solution.py:43
  61.5 1.7 collective-permute-start.11
  63.2 4.7 %collective-permute-start.9 = (f32[1,1,4,64]{3,2,1,0:T(4,128)S(1)}, f32[1,1,4,64]{3,2,1,0:T(4,128)S(1)}, u32[]{:S(2)}, u32[]{:S(2)}) collective-permute-start(f32[1,1,4,64]{3,2,1,0:T(4,128)S(1)} %get-tuple-element.72), channel_id=1, source_target_pairs={{1,0},{2,1},{3,2},{4,3},{5,4},{6,5},{7,6},{0,7},{9,8},{10,9},{11,1... | collective-permute-start | bytes 3080 | tf_op jit(solution)/shard_map/ppermute | solution.py:19
  68.0 1.5 collective-permute-done.8
  69.6 9.6 %gather_fusion.2 = f32[1024]{0:T(1024)S(1)} fusion(f32[2,4,128]{2,1,0:T(4,128)S(1)} %fusion.61, s32[1024]{0:T(1024)S(1)} %bitcast.198), kind=kCustom, calls=%fused_computation.2.clone | custom fusion | bytes 20480 | tf_op jit(solution)/shard_map/jit(take_along_axis)/gather | solution.py:43
  79.6 1.8 collective-permute-start.15
  81.3 4.7 %collective-permute-start.13 = (f32[1,1,4,64]{3,2,1,0:T(4,128)S(1)}, f32[1,1,4,64]{3,2,1,0:T(4,128)S(1)}, u32[]{:S(2)}, u32[]{:S(2)}) collective-permute-start(f32[1,1,4,64]{3,2,1,0:T(4,128)S(1)} %get-tuple-element.68), channel_id=1, source_target_pairs={{1,0},{2,1},{3,2},{4,3},{5,4},{6,5},{7,6},{0,7},{9,8},{10,9},{11,1... | collective-permute-start | bytes 3080 | tf_op jit(solution)/shard_map/ppermute | solution.py:19
  86.1 1.5 collective-permute-done.12
  87.7 9.6 %gather_fusion.3 = f32[1024]{0:T(1024)S(1)} fusion(f32[2,4,128]{2,1,0:T(4,128)S(1)} %fusion.57, s32[1024]{0:T(1024)S(1)} %bitcast.199), kind=kCustom, calls=%fused_computation.3.clone | custom fusion | bytes 20480 | tf_op jit(solution)/shard_map/jit(take_along_axis)/gather | solution.py:43
  97.4 1.7 collective-permute-start.19
  99.2 4.7 %collective-permute-start.17 = (f32[1,1,4,64]{3,2,1,0:T(4,128)S(1)}, f32[1,1,4,64]{3,2,1,0:T(4,128)S(1)}, u32[]{:S(2)}, u32[]{:S(2)}) collective-permute-start(f32[1,1,4,64]{3,2,1,0:T(4,128)S(1)} %get-tuple-element.64), channel_id=1, source_target_pairs={{1,0},{2,1},{3,2},{4,3},{5,4},{6,5},{7,6},{0,7},{9,8},{10,9},{11,1... | collective-permute-start | bytes 3080 | tf_op jit(solution)/shard_map/ppermute | solution.py:19
  104.0 1.5 collective-permute-done.16
  105.5 9.6 %gather_fusion.4 = f32[1024]{0:T(1024)S(1)} fusion(f32[2,4,128]{2,1,0:T(4,128)S(1)} %fusion.53, s32[1024]{0:T(1024)S(1)} %bitcast.200), kind=kCustom, calls=%fused_computation.4.clone | custom fusion | bytes 20480 | tf_op jit(solution)/shard_map/jit(take_along_axis)/gather | solution.py:43
  115.3 21.0 %all-gather.1 = f32[8,2,4]{2,1,0:T(2,128)S(1)} all-gather(f32[1,2,4]{2,1,0:T(2,128)S(1)} %bitcast.257), channel_id=1, replica_groups=mesh['srow'=4,'scol'=8] {'scol'}, dimensions={0}, use_global_device_ids=true | all-gather | bytes 288 | tf_op jit(solution)/shard_map/all_gather | solution.py:55
  136.8 1.7 collective-permute-start.23
  138.6 4.7 %collective-permute-start.21 = (f32[1,1,4,64]{3,2,1,0:T(4,128)S(1)}, f32[1,1,4,64]{3,2,1,0:T(4,128)S(1)}, u32[]{:S(2)}, u32[]{:S(2)}) collective-permute-start(f32[1,1,4,64]{3,2,1,0:T(4,128)S(1)} %get-tuple-element.60), channel_id=1, source_target_pairs={{1,0},{2,1},{3,2},{4,3},{5,4},{6,5},{7,6},{0,7},{9,8},{10,9},{11,1... | collective-permute-start | bytes 3080 | tf_op jit(solution)/shard_map/ppermute | solution.py:19
  143.4 1.5 collective-permute-done.20
  144.9 9.6 %gather_fusion.5 = f32[1024]{0:T(1024)S(1)} fusion(f32[2,4,128]{2,1,0:T(4,128)S(1)} %fusion.49, s32[1024]{0:T(1024)S(1)} %bitcast.201), kind=kCustom, calls=%fused_computation.5.clone | custom fusion | bytes 20480 | tf_op jit(solution)/shard_map/jit(take_along_axis)/gather | solution.py:43
  154.7 40.2 %all-reduce.2 = (f32[4]{0:T(128)S(1)}, f32[4]{0:T(128)S(1)}) all-reduce(f32[4]{0:T(128)S(1)} %get-tuple-element.8, f32[4]{0:T(128)S(1)} %get-tuple-element.7), channel_id=1, replica_groups=mesh['srow'=4,'scol'=8] {'srow','scol'}, use_global_device_ids=true, to_apply=%region_1.3 | all-reduce | flops 8 | bytes 64 | tf_op jit(solution)/shard_map/psum | solution.py:68
  195.1 1.7 collective-permute-start.27
  196.8 2.3 collective-permute-start.24
  199.1 2.4 collective-permute-start.25
  201.6 1.5 collective-permute-done.24
  203.2 9.6 %gather_fusion.6 = f32[1024]{0:T(1024)S(1)} fusion(f32[2,4,128]{2,1,0:T(4,128)S(1)} %fusion.45, s32[1024]{0:T(1024)S(1)} %bitcast.202), kind=kCustom, calls=%fused_computation.6.clone | custom fusion | bytes 20480 | tf_op jit(solution)/shard_map/jit(take_along_axis)/gather | solution.py:43
  213.2 1.8 collective-permute-start.31
  214.9 1.8 collective-permute-start.28
  216.7 2.9 collective-permute-start.29
  219.7 1.5 collective-permute-done.28
  221.3 9.6 %gather_fusion.7 = f32[1024]{0:T(1024)S(1)} fusion(f32[2,4,128]{2,1,0:T(4,128)S(1)} %fusion.41, s32[1024]{0:T(1024)S(1)} %bitcast.203), kind=kCustom, calls=%fused_computation.7.clone | custom fusion | bytes 20480 | tf_op jit(solution)/shard_map/jit(take_along_axis)/gather | solution.py:43
  231.0 1.7 collective-permute-start.35
  234.1 3.4 collective-permute-start.33
  237.6 1.5 collective-permute-done.32
  239.1 9.6 %gather_fusion.8 = f32[1024]{0:T(1024)S(1)} fusion(f32[2,4,128]{2,1,0:T(4,128)S(1)} %fusion.37, s32[1024]{0:T(1024)S(1)} %bitcast.204), kind=kCustom, calls=%fused_computation.8.clone | custom fusion | bytes 20480 | tf_op jit(solution)/shard_map/jit(take_along_axis)/gather | solution.py:43
  248.9 21.0 %all-gather.2 = f32[8,2,4]{2,1,0:T(2,128)S(1)} all-gather(f32[1,2,4]{2,1,0:T(2,128)S(1)} %bitcast.258), channel_id=1, replica_groups=mesh['srow'=4,'scol'=8] {'scol'}, dimensions={0}, use_global_device_ids=true | all-gather | bytes 288 | tf_op jit(solution)/shard_map/all_gather | solution.py:55
  270.4 1.7 collective-permute-start.39
  272.2 4.7 %collective-permute-start.37 = (f32[1,1,4,64]{3,2,1,0:T(4,128)S(1)}, f32[1,1,4,64]{3,2,1,0:T(4,128)S(1)}, u32[]{:S(2)}, u32[]{:S(2)}) collective-permute-start(f32[1,1,4,64]{3,2,1,0:T(4,128)S(1)} %get-tuple-element.44), channel_id=1, source_target_pairs={{1,0},{2,1},{3,2},{4,3},{5,4},{6,5},{7,6},{0,7},{9,8},{10,9},{11,1... | collective-permute-start | bytes 3080 | tf_op jit(solution)/shard_map/ppermute | solution.py:19
  278.5 9.6 %gather_fusion.9 = f32[1024]{0:T(1024)S(1)} fusion(f32[2,4,128]{2,1,0:T(4,128)S(1)} %fusion.33, s32[1024]{0:T(1024)S(1)} %bitcast.205), kind=kCustom, calls=%fused_computation.9.clone | custom fusion | bytes 20480 | tf_op jit(solution)/shard_map/jit(take_along_axis)/gather | solution.py:43
  288.3 40.8 %all-reduce.1 = (f32[4]{0:T(128)S(1)}, f32[4]{0:T(128)S(1)}) all-reduce(f32[4]{0:T(128)S(1)} %get-tuple-element.6, f32[4]{0:T(128)S(1)} %get-tuple-element.5), channel_id=1, replica_groups=mesh['srow'=4,'scol'=8] {'srow','scol'}, use_global_device_ids=true, to_apply=%region_5.7 | all-reduce | flops 8 | bytes 64 | tf_op jit(solution)/shard_map/psum | solution.py:68
  329.3 1.8 collective-permute-start.43
  331.1 2.3 collective-permute-start.40
  333.3 2.4 collective-permute-start.41
  337.4 9.6 %gather_fusion.10 = f32[1024]{0:T(1024)S(1)} fusion(f32[2,4,128]{2,1,0:T(4,128)S(1)} %fusion.29, s32[1024]{0:T(1024)S(1)} %bitcast.206), kind=kCustom, calls=%fused_computation.10.clone | custom fusion | bytes 20480 | tf_op jit(solution)/shard_map/jit(take_along_axis)/gather | solution.py:43
  347.4 1.8 collective-permute-start.47
  349.2 1.8 collective-permute-start.44
  351.0 2.9 collective-permute-start.45
  354.0 1.5 collective-permute-done.44
  355.5 9.6 %gather_fusion.11 = f32[1024]{0:T(1024)S(1)} fusion(f32[2,4,128]{2,1,0:T(4,128)S(1)} %fusion.25, s32[1024]{0:T(1024)S(1)} %bitcast.207), kind=kCustom, calls=%fused_computation.11.clone | custom fusion | bytes 20480 | tf_op jit(solution)/shard_map/jit(take_along_axis)/gather | solution.py:43
  365.3 1.7 collective-permute-start.51
  368.4 3.4 collective-permute-start.49
  371.8 1.5 collective-permute-done.48
  373.4 9.6 %gather_fusion.12 = f32[1024]{0:T(1024)S(1)} fusion(f32[2,4,128]{2,1,0:T(4,128)S(1)} %fusion.21, s32[1024]{0:T(1024)S(1)} %bitcast.208), kind=kCustom, calls=%fused_computation.12.clone | custom fusion | bytes 20480 | tf_op jit(solution)/shard_map/jit(take_along_axis)/gather | solution.py:43
  383.1 21.0 %all-gather.3 = f32[8,2,4]{2,1,0:T(2,128)S(1)} all-gather(f32[1,2,4]{2,1,0:T(2,128)S(1)} %bitcast.259), channel_id=1, replica_groups=mesh['srow'=4,'scol'=8] {'scol'}, dimensions={0}, use_global_device_ids=true | all-gather | bytes 288 | tf_op jit(solution)/shard_map/all_gather | solution.py:55
  404.7 1.7 collective-permute-start.55
  406.4 4.7 %collective-permute-start.53 = (f32[1,1,4,64]{3,2,1,0:T(4,128)S(1)}, f32[1,1,4,64]{3,2,1,0:T(4,128)S(1)}, u32[]{:S(2)}, u32[]{:S(2)}) collective-permute-start(f32[1,1,4,64]{3,2,1,0:T(4,128)S(1)} %get-tuple-element.28), channel_id=1, source_target_pairs={{1,0},{2,1},{3,2},{4,3},{5,4},{6,5},{7,6},{0,7},{9,8},{10,9},{11,1... | collective-permute-start | bytes 3080 | tf_op jit(solution)/shard_map/ppermute | solution.py:19
  412.8 9.6 %gather_fusion.13 = f32[1024]{0:T(1024)S(1)} fusion(f32[2,4,128]{2,1,0:T(4,128)S(1)} %fusion.17, s32[1024]{0:T(1024)S(1)} %bitcast.209), kind=kCustom, calls=%fused_computation.13.clone | custom fusion | bytes 20480 | tf_op jit(solution)/shard_map/jit(take_along_axis)/gather | solution.py:43
  422.5 40.8 %all-reduce = (f32[4]{0:T(128)S(1)}, f32[4]{0:T(128)S(1)}) all-reduce(f32[4]{0:T(128)S(1)} %get-tuple-element.4, f32[4]{0:T(128)S(1)} %get-tuple-element.3), channel_id=1, replica_groups=mesh['srow'=4,'scol'=8] {'srow','scol'}, use_global_device_ids=true, to_apply=%region_9.11 | all-reduce | flops 8 | bytes 64 | tf_op jit(solution)/shard_map/psum | solution.py:68
  (171 shorter events, 19.1 us)
Async XLA Ops:
  0.6 42.6 %copy-start = (f32[1,2,128,128]{3,2,1,0:T(8,128)S(1)}, f32[1,2,128,128]{3,2,1,0:T(8,128)}, u32[]{:S(2)}) copy-start(f32[1,2,128,128]{3,2,1,0:T(8,128)} %param.9) | copy-start | bytes 393220
  0.6 3.3 copy-start.2
  1.5 7.9 %collective-permute-start.2 = (f32[1,2,4,64]{3,2,1,0:T(4,128)S(1)}, f32[1,2,4,64]{3,2,1,0:T(4,128)S(1)}, u32[]{:S(2)}, u32[]{:S(2)}) collective-permute-start(f32[1,2,4,64]{3,2,1,0:T(4,128)S(1)} %get-tuple-element.77), channel_id=1, source_target_pairs={{0,8},{8,16},{16,24},{24,0},{1,9},{9,17},{17,25},{25,1},{2,10},{10... | collective-permute-start | bytes 6152 | tf_op jit(solution)/shard_map/ppermute | solution.py:17
  2.0 8.8 %collective-permute-start.3 = (f32[1,2,4,64]{3,2,1,0:T(4,128)S(1)}, f32[1,2,4,64]{3,2,1,0:T(4,128)S(1)}, u32[]{:S(2)}, u32[]{:S(2)}) collective-permute-start(f32[1,2,4,64]{3,2,1,0:T(4,128)S(1)} %get-tuple-element.77), channel_id=1, source_target_pairs={{8,0},{16,8},{24,16},{0,24},{9,1},{17,9},{25,17},{1,25},{10,2},{18... | collective-permute-start | bytes 6152 | tf_op jit(solution)/shard_map/ppermute | solution.py:19
  4.0 6.9 %collective-permute-start = (f32[1,1,4,64]{3,2,1,0:T(4,128)S(1)}, f32[1,1,4,64]{3,2,1,0:T(4,128)S(1)}, u32[]{:S(2)}, u32[]{:S(2)}) collective-permute-start(f32[1,1,4,64]{3,2,1,0:T(4,128)S(1)} %get-tuple-element.79), channel_id=1, source_target_pairs={{0,1},{1,2},{2,3},{3,4},{4,5},{5,6},{6,7},{7,0},{8,9},{9,10},{10,1... | collective-permute-start | bytes 3080 | tf_op jit(solution)/shard_map/ppermute | solution.py:17
  6.2 3.1 copy-start.5
  6.2 4.6 collective-permute-start.1
  20.5 0.7 copy-start.3
  42.4 0.7 copy-start.4
  43.6 6.5 %collective-permute-start.6 = (f32[1,2,4,64]{3,2,1,0:T(4,128)S(1)}, f32[1,2,4,64]{3,2,1,0:T(4,128)S(1)}, u32[]{:S(2)}, u32[]{:S(2)}) collective-permute-start(f32[1,2,4,64]{3,2,1,0:T(4,128)S(1)} %get-tuple-element.73), channel_id=1, source_target_pairs={{0,8},{8,16},{16,24},{24,0},{1,9},{9,17},{17,25},{25,1},{2,10},{10... | collective-permute-start | bytes 6152 | tf_op jit(solution)/shard_map/ppermute | solution.py:17
  43.6 8.0 %collective-permute-start.7 = (f32[1,2,4,64]{3,2,1,0:T(4,128)S(1)}, f32[1,2,4,64]{3,2,1,0:T(4,128)S(1)}, u32[]{:S(2)}, u32[]{:S(2)}) collective-permute-start(f32[1,2,4,64]{3,2,1,0:T(4,128)S(1)} %get-tuple-element.73), channel_id=1, source_target_pairs={{8,0},{16,8},{24,16},{0,24},{9,1},{17,9},{25,17},{1,25},{10,2},{18... | collective-permute-start | bytes 6152 | tf_op jit(solution)/shard_map/ppermute | solution.py:19
  45.4 6.3 %collective-permute-start.4 = (f32[1,1,4,64]{3,2,1,0:T(4,128)S(1)}, f32[1,1,4,64]{3,2,1,0:T(4,128)S(1)}, u32[]{:S(2)}, u32[]{:S(2)}) collective-permute-start(f32[1,1,4,64]{3,2,1,0:T(4,128)S(1)} %get-tuple-element.75), channel_id=1, source_target_pairs={{0,1},{1,2},{2,3},{3,4},{4,5},{5,6},{6,7},{7,0},{8,9},{9,10},{10,1... | collective-permute-start | bytes 3080 | tf_op jit(solution)/shard_map/ppermute | solution.py:17
  45.4 6.3 %collective-permute-start.5 = (f32[1,1,4,64]{3,2,1,0:T(4,128)S(1)}, f32[1,1,4,64]{3,2,1,0:T(4,128)S(1)}, u32[]{:S(2)}, u32[]{:S(2)}) collective-permute-start(f32[1,1,4,64]{3,2,1,0:T(4,128)S(1)} %get-tuple-element.76), channel_id=1, source_target_pairs={{1,0},{2,1},{3,2},{4,3},{5,4},{6,5},{7,6},{0,7},{9,8},{10,9},{11,1... | collective-permute-start | bytes 3080 | tf_op jit(solution)/shard_map/ppermute | solution.py:19
  61.4 6.5 %collective-permute-start.10 = (f32[1,2,4,64]{3,2,1,0:T(4,128)S(1)}, f32[1,2,4,64]{3,2,1,0:T(4,128)S(1)}, u32[]{:S(2)}, u32[]{:S(2)}) collective-permute-start(f32[1,2,4,64]{3,2,1,0:T(4,128)S(1)} %get-tuple-element.69), channel_id=1, source_target_pairs={{0,8},{8,16},{16,24},{24,0},{1,9},{9,17},{17,25},{25,1},{2,10},{10... | collective-permute-start | bytes 6152 | tf_op jit(solution)/shard_map/ppermute | solution.py:17
  61.5 8.0 %collective-permute-start.11 = (f32[1,2,4,64]{3,2,1,0:T(4,128)S(1)}, f32[1,2,4,64]{3,2,1,0:T(4,128)S(1)}, u32[]{:S(2)}, u32[]{:S(2)}) collective-permute-start(f32[1,2,4,64]{3,2,1,0:T(4,128)S(1)} %get-tuple-element.69), channel_id=1, source_target_pairs={{8,0},{16,8},{24,16},{0,24},{9,1},{17,9},{25,17},{1,25},{10,2},{18... | collective-permute-start | bytes 6152 | tf_op jit(solution)/shard_map/ppermute | solution.py:19
  63.2 6.3 %collective-permute-start.8 = (f32[1,1,4,64]{3,2,1,0:T(4,128)S(1)}, f32[1,1,4,64]{3,2,1,0:T(4,128)S(1)}, u32[]{:S(2)}, u32[]{:S(2)}) collective-permute-start(f32[1,1,4,64]{3,2,1,0:T(4,128)S(1)} %get-tuple-element.71), channel_id=1, source_target_pairs={{0,1},{1,2},{2,3},{3,4},{4,5},{5,6},{6,7},{7,0},{8,9},{9,10},{10,1... | collective-permute-start | bytes 3080 | tf_op jit(solution)/shard_map/ppermute | solution.py:17
  63.2 6.3 %collective-permute-start.9 = (f32[1,1,4,64]{3,2,1,0:T(4,128)S(1)}, f32[1,1,4,64]{3,2,1,0:T(4,128)S(1)}, u32[]{:S(2)}, u32[]{:S(2)}) collective-permute-start(f32[1,1,4,64]{3,2,1,0:T(4,128)S(1)} %get-tuple-element.72), channel_id=1, source_target_pairs={{1,0},{2,1},{3,2},{4,3},{5,4},{6,5},{7,6},{0,7},{9,8},{10,9},{11,1... | collective-permute-start | bytes 3080 | tf_op jit(solution)/shard_map/ppermute | solution.py:19
  69.6 9.6 %copy-start.1 = (f32[1,2,128,128]{3,2,1,0:T(8,128)S(1)}, f32[1,2,128,128]{3,2,1,0:T(8,128)}, u32[]{:S(2)}) copy-start(f32[1,2,128,128]{3,2,1,0:T(8,128)} %param.10) | copy-start | bytes 393220
  79.6 6.5 %collective-permute-start.14 = (f32[1,2,4,64]{3,2,1,0:T(4,128)S(1)}, f32[1,2,4,64]{3,2,1,0:T(4,128)S(1)}, u32[]{:S(2)}, u32[]{:S(2)}) collective-permute-start(f32[1,2,4,64]{3,2,1,0:T(4,128)S(1)} %get-tuple-element.65), channel_id=1, source_target_pairs={{0,8},{8,16},{16,24},{24,0},{1,9},{9,17},{17,25},{25,1},{2,10},{10... | collective-permute-start | bytes 6152 | tf_op jit(solution)/shard_map/ppermute | solution.py:17
  79.6 8.0 %collective-permute-start.15 = (f32[1,2,4,64]{3,2,1,0:T(4,128)S(1)}, f32[1,2,4,64]{3,2,1,0:T(4,128)S(1)}, u32[]{:S(2)}, u32[]{:S(2)}) collective-permute-start(f32[1,2,4,64]{3,2,1,0:T(4,128)S(1)} %get-tuple-element.65), channel_id=1, source_target_pairs={{8,0},{16,8},{24,16},{0,24},{9,1},{17,9},{25,17},{1,25},{10,2},{18... | collective-permute-start | bytes 6152 | tf_op jit(solution)/shard_map/ppermute | solution.py:19
  81.3 6.3 %collective-permute-start.12 = (f32[1,1,4,64]{3,2,1,0:T(4,128)S(1)}, f32[1,1,4,64]{3,2,1,0:T(4,128)S(1)}, u32[]{:S(2)}, u32[]{:S(2)}) collective-permute-start(f32[1,1,4,64]{3,2,1,0:T(4,128)S(1)} %get-tuple-element.67), channel_id=1, source_target_pairs={{0,1},{1,2},{2,3},{3,4},{4,5},{5,6},{6,7},{7,0},{8,9},{9,10},{10,1... | collective-permute-start | bytes 3080 | tf_op jit(solution)/shard_map/ppermute | solution.py:17
  81.3 6.3 %collective-permute-start.13 = (f32[1,1,4,64]{3,2,1,0:T(4,128)S(1)}, f32[1,1,4,64]{3,2,1,0:T(4,128)S(1)}, u32[]{:S(2)}, u32[]{:S(2)}) collective-permute-start(f32[1,1,4,64]{3,2,1,0:T(4,128)S(1)} %get-tuple-element.68), channel_id=1, source_target_pairs={{1,0},{2,1},{3,2},{4,3},{5,4},{6,5},{7,6},{0,7},{9,8},{10,9},{11,1... | collective-permute-start | bytes 3080 | tf_op jit(solution)/shard_map/ppermute | solution.py:19
  97.4 6.5 %collective-permute-start.18 = (f32[1,2,4,64]{3,2,1,0:T(4,128)S(1)}, f32[1,2,4,64]{3,2,1,0:T(4,128)S(1)}, u32[]{:S(2)}, u32[]{:S(2)}) collective-permute-start(f32[1,2,4,64]{3,2,1,0:T(4,128)S(1)} %get-tuple-element.61), channel_id=1, source_target_pairs={{0,8},{8,16},{16,24},{24,0},{1,9},{9,17},{17,25},{25,1},{2,10},{10... | collective-permute-start | bytes 6152 | tf_op jit(solution)/shard_map/ppermute | solution.py:17
  97.4 8.0 %collective-permute-start.19 = (f32[1,2,4,64]{3,2,1,0:T(4,128)S(1)}, f32[1,2,4,64]{3,2,1,0:T(4,128)S(1)}, u32[]{:S(2)}, u32[]{:S(2)}) collective-permute-start(f32[1,2,4,64]{3,2,1,0:T(4,128)S(1)} %get-tuple-element.61), channel_id=1, source_target_pairs={{8,0},{16,8},{24,16},{0,24},{9,1},{17,9},{25,17},{1,25},{10,2},{18... | collective-permute-start | bytes 6152 | tf_op jit(solution)/shard_map/ppermute | solution.py:19
  99.2 6.3 %collective-permute-start.16 = (f32[1,1,4,64]{3,2,1,0:T(4,128)S(1)}, f32[1,1,4,64]{3,2,1,0:T(4,128)S(1)}, u32[]{:S(2)}, u32[]{:S(2)}) collective-permute-start(f32[1,1,4,64]{3,2,1,0:T(4,128)S(1)} %get-tuple-element.63), channel_id=1, source_target_pairs={{0,1},{1,2},{2,3},{3,4},{4,5},{5,6},{6,7},{7,0},{8,9},{9,10},{10,1... | collective-permute-start | bytes 3080 | tf_op jit(solution)/shard_map/ppermute | solution.py:17
  99.2 6.3 %collective-permute-start.17 = (f32[1,1,4,64]{3,2,1,0:T(4,128)S(1)}, f32[1,1,4,64]{3,2,1,0:T(4,128)S(1)}, u32[]{:S(2)}, u32[]{:S(2)}) collective-permute-start(f32[1,1,4,64]{3,2,1,0:T(4,128)S(1)} %get-tuple-element.64), channel_id=1, source_target_pairs={{1,0},{2,1},{3,2},{4,3},{5,4},{6,5},{7,6},{0,7},{9,8},{10,9},{11,1... | collective-permute-start | bytes 3080 | tf_op jit(solution)/shard_map/ppermute | solution.py:19
  136.8 6.5 %collective-permute-start.22 = (f32[1,2,4,64]{3,2,1,0:T(4,128)S(1)}, f32[1,2,4,64]{3,2,1,0:T(4,128)S(1)}, u32[]{:S(2)}, u32[]{:S(2)}) collective-permute-start(f32[1,2,4,64]{3,2,1,0:T(4,128)S(1)} %get-tuple-element.57), channel_id=1, source_target_pairs={{0,8},{8,16},{16,24},{24,0},{1,9},{9,17},{17,25},{25,1},{2,10},{10... | collective-permute-start | bytes 6152 | tf_op jit(solution)/shard_map/ppermute | solution.py:17
  136.8 8.0 %collective-permute-start.23 = (f32[1,2,4,64]{3,2,1,0:T(4,128)S(1)}, f32[1,2,4,64]{3,2,1,0:T(4,128)S(1)}, u32[]{:S(2)}, u32[]{:S(2)}) collective-permute-start(f32[1,2,4,64]{3,2,1,0:T(4,128)S(1)} %get-tuple-element.57), channel_id=1, source_target_pairs={{8,0},{16,8},{24,16},{0,24},{9,1},{17,9},{25,17},{1,25},{10,2},{18... | collective-permute-start | bytes 6152 | tf_op jit(solution)/shard_map/ppermute | solution.py:19
  138.6 6.3 %collective-permute-start.20 = (f32[1,1,4,64]{3,2,1,0:T(4,128)S(1)}, f32[1,1,4,64]{3,2,1,0:T(4,128)S(1)}, u32[]{:S(2)}, u32[]{:S(2)}) collective-permute-start(f32[1,1,4,64]{3,2,1,0:T(4,128)S(1)} %get-tuple-element.59), channel_id=1, source_target_pairs={{0,1},{1,2},{2,3},{3,4},{4,5},{5,6},{6,7},{7,0},{8,9},{9,10},{10,1... | collective-permute-start | bytes 3080 | tf_op jit(solution)/shard_map/ppermute | solution.py:17
  138.6 6.3 %collective-permute-start.21 = (f32[1,1,4,64]{3,2,1,0:T(4,128)S(1)}, f32[1,1,4,64]{3,2,1,0:T(4,128)S(1)}, u32[]{:S(2)}, u32[]{:S(2)}) collective-permute-start(f32[1,1,4,64]{3,2,1,0:T(4,128)S(1)} %get-tuple-element.60), channel_id=1, source_target_pairs={{1,0},{2,1},{3,2},{4,3},{5,4},{6,5},{7,6},{0,7},{9,8},{10,9},{11,1... | collective-permute-start | bytes 3080 | tf_op jit(solution)/shard_map/ppermute | solution.py:19
  195.1 6.5 %collective-permute-start.26 = (f32[1,2,4,64]{3,2,1,0:T(4,128)S(1)}, f32[1,2,4,64]{3,2,1,0:T(4,128)S(1)}, u32[]{:S(2)}, u32[]{:S(2)}) collective-permute-start(f32[1,2,4,64]{3,2,1,0:T(4,128)S(1)} %get-tuple-element.53), channel_id=1, source_target_pairs={{0,8},{8,16},{16,24},{24,0},{1,9},{9,17},{17,25},{25,1},{2,10},{10... | collective-permute-start | bytes 6152 | tf_op jit(solution)/shard_map/ppermute | solution.py:17
  195.1 8.0 %collective-permute-start.27 = (f32[1,2,4,64]{3,2,1,0:T(4,128)S(1)}, f32[1,2,4,64]{3,2,1,0:T(4,128)S(1)}, u32[]{:S(2)}, u32[]{:S(2)}) collective-permute-start(f32[1,2,4,64]{3,2,1,0:T(4,128)S(1)} %get-tuple-element.53), channel_id=1, source_target_pairs={{8,0},{16,8},{24,16},{0,24},{9,1},{17,9},{25,17},{1,25},{10,2},{18... | collective-permute-start | bytes 6152 | tf_op jit(solution)/shard_map/ppermute | solution.py:19
  196.8 6.3 %collective-permute-start.24 = (f32[1,1,4,64]{3,2,1,0:T(4,128)S(1)}, f32[1,1,4,64]{3,2,1,0:T(4,128)S(1)}, u32[]{:S(2)}, u32[]{:S(2)}) collective-permute-start(f32[1,1,4,64]{3,2,1,0:T(4,128)S(1)} %get-tuple-element.55), channel_id=1, source_target_pairs={{0,1},{1,2},{2,3},{3,4},{4,5},{5,6},{6,7},{7,0},{8,9},{9,10},{10,1... | collective-permute-start | bytes 3080 | tf_op jit(solution)/shard_map/ppermute | solution.py:17
  199.1 4.0 collective-permute-start.25
  213.2 6.5 %collective-permute-start.30 = (f32[1,2,4,64]{3,2,1,0:T(4,128)S(1)}, f32[1,2,4,64]{3,2,1,0:T(4,128)S(1)}, u32[]{:S(2)}, u32[]{:S(2)}) collective-permute-start(f32[1,2,4,64]{3,2,1,0:T(4,128)S(1)} %get-tuple-element.49), channel_id=1, source_target_pairs={{0,8},{8,16},{16,24},{24,0},{1,9},{9,17},{17,25},{25,1},{2,10},{10... | collective-permute-start | bytes 6152 | tf_op jit(solution)/shard_map/ppermute | solution.py:17
  213.2 8.0 %collective-permute-start.31 = (f32[1,2,4,64]{3,2,1,0:T(4,128)S(1)}, f32[1,2,4,64]{3,2,1,0:T(4,128)S(1)}, u32[]{:S(2)}, u32[]{:S(2)}) collective-permute-start(f32[1,2,4,64]{3,2,1,0:T(4,128)S(1)} %get-tuple-element.49), channel_id=1, source_target_pairs={{8,0},{16,8},{24,16},{0,24},{9,1},{17,9},{25,17},{1,25},{10,2},{18... | collective-permute-start | bytes 6152 | tf_op jit(solution)/shard_map/ppermute | solution.py:19
  214.9 6.3 %collective-permute-start.28 = (f32[1,1,4,64]{3,2,1,0:T(4,128)S(1)}, f32[1,1,4,64]{3,2,1,0:T(4,128)S(1)}, u32[]{:S(2)}, u32[]{:S(2)}) collective-permute-start(f32[1,1,4,64]{3,2,1,0:T(4,128)S(1)} %get-tuple-element.51), channel_id=1, source_target_pairs={{0,1},{1,2},{2,3},{3,4},{4,5},{5,6},{6,7},{7,0},{8,9},{9,10},{10,1... | collective-permute-start | bytes 3080 | tf_op jit(solution)/shard_map/ppermute | solution.py:17
  216.7 4.5 collective-permute-start.29
  231.0 6.5 %collective-permute-start.34 = (f32[1,2,4,64]{3,2,1,0:T(4,128)S(1)}, f32[1,2,4,64]{3,2,1,0:T(4,128)S(1)}, u32[]{:S(2)}, u32[]{:S(2)}) collective-permute-start(f32[1,2,4,64]{3,2,1,0:T(4,128)S(1)} %get-tuple-element.45), channel_id=1, source_target_pairs={{0,8},{8,16},{16,24},{24,0},{1,9},{9,17},{17,25},{25,1},{2,10},{10... | collective-permute-start | bytes 6152 | tf_op jit(solution)/shard_map/ppermute | solution.py:17
  231.0 8.0 %collective-permute-start.35 = (f32[1,2,4,64]{3,2,1,0:T(4,128)S(1)}, f32[1,2,4,64]{3,2,1,0:T(4,128)S(1)}, u32[]{:S(2)}, u32[]{:S(2)}) collective-permute-start(f32[1,2,4,64]{3,2,1,0:T(4,128)S(1)} %get-tuple-element.45), channel_id=1, source_target_pairs={{8,0},{16,8},{24,16},{0,24},{9,1},{17,9},{25,17},{1,25},{10,2},{18... | collective-permute-start | bytes 6152 | tf_op jit(solution)/shard_map/ppermute | solution.py:19
  232.8 6.3 %collective-permute-start.32 = (f32[1,1,4,64]{3,2,1,0:T(4,128)S(1)}, f32[1,1,4,64]{3,2,1,0:T(4,128)S(1)}, u32[]{:S(2)}, u32[]{:S(2)}) collective-permute-start(f32[1,1,4,64]{3,2,1,0:T(4,128)S(1)} %get-tuple-element.47), channel_id=1, source_target_pairs={{0,1},{1,2},{2,3},{3,4},{4,5},{5,6},{6,7},{7,0},{8,9},{9,10},{10,1... | collective-permute-start | bytes 3080 | tf_op jit(solution)/shard_map/ppermute | solution.py:17
  234.1 4.9 %collective-permute-start.33 = (f32[1,1,4,64]{3,2,1,0:T(4,128)S(1)}, f32[1,1,4,64]{3,2,1,0:T(4,128)S(1)}, u32[]{:S(2)}, u32[]{:S(2)}) collective-permute-start(f32[1,1,4,64]{3,2,1,0:T(4,128)S(1)} %get-tuple-element.48), channel_id=1, source_target_pairs={{1,0},{2,1},{3,2},{4,3},{5,4},{6,5},{7,6},{0,7},{9,8},{10,9},{11,1... | collective-permute-start | bytes 3080 | tf_op jit(solution)/shard_map/ppermute | solution.py:19
  270.4 6.5 %collective-permute-start.38 = (f32[1,2,4,64]{3,2,1,0:T(4,128)S(1)}, f32[1,2,4,64]{3,2,1,0:T(4,128)S(1)}, u32[]{:S(2)}, u32[]{:S(2)}) collective-permute-start(f32[1,2,4,64]{3,2,1,0:T(4,128)S(1)} %get-tuple-element.41), channel_id=1, source_target_pairs={{0,8},{8,16},{16,24},{24,0},{1,9},{9,17},{17,25},{25,1},{2,10},{10... | collective-permute-start | bytes 6152 | tf_op jit(solution)/shard_map/ppermute | solution.py:17
  270.4 8.0 %collective-permute-start.39 = (f32[1,2,4,64]{3,2,1,0:T(4,128)S(1)}, f32[1,2,4,64]{3,2,1,0:T(4,128)S(1)}, u32[]{:S(2)}, u32[]{:S(2)}) collective-permute-start(f32[1,2,4,64]{3,2,1,0:T(4,128)S(1)} %get-tuple-element.41), channel_id=1, source_target_pairs={{8,0},{16,8},{24,16},{0,24},{9,1},{17,9},{25,17},{1,25},{10,2},{18... | collective-permute-start | bytes 6152 | tf_op jit(solution)/shard_map/ppermute | solution.py:19
  272.2 6.3 %collective-permute-start.36 = (f32[1,1,4,64]{3,2,1,0:T(4,128)S(1)}, f32[1,1,4,64]{3,2,1,0:T(4,128)S(1)}, u32[]{:S(2)}, u32[]{:S(2)}) collective-permute-start(f32[1,1,4,64]{3,2,1,0:T(4,128)S(1)} %get-tuple-element.43), channel_id=1, source_target_pairs={{0,1},{1,2},{2,3},{3,4},{4,5},{5,6},{6,7},{7,0},{8,9},{9,10},{10,1... | collective-permute-start | bytes 3080 | tf_op jit(solution)/shard_map/ppermute | solution.py:17
  272.2 6.3 %collective-permute-start.37 = (f32[1,1,4,64]{3,2,1,0:T(4,128)S(1)}, f32[1,1,4,64]{3,2,1,0:T(4,128)S(1)}, u32[]{:S(2)}, u32[]{:S(2)}) collective-permute-start(f32[1,1,4,64]{3,2,1,0:T(4,128)S(1)} %get-tuple-element.44), channel_id=1, source_target_pairs={{1,0},{2,1},{3,2},{4,3},{5,4},{6,5},{7,6},{0,7},{9,8},{10,9},{11,1... | collective-permute-start | bytes 3080 | tf_op jit(solution)/shard_map/ppermute | solution.py:19
  329.3 6.5 %collective-permute-start.42 = (f32[1,2,4,64]{3,2,1,0:T(4,128)S(1)}, f32[1,2,4,64]{3,2,1,0:T(4,128)S(1)}, u32[]{:S(2)}, u32[]{:S(2)}) collective-permute-start(f32[1,2,4,64]{3,2,1,0:T(4,128)S(1)} %get-tuple-element.37), channel_id=1, source_target_pairs={{0,8},{8,16},{16,24},{24,0},{1,9},{9,17},{17,25},{25,1},{2,10},{10... | collective-permute-start | bytes 6152 | tf_op jit(solution)/shard_map/ppermute | solution.py:17
  329.3 8.0 %collective-permute-start.43 = (f32[1,2,4,64]{3,2,1,0:T(4,128)S(1)}, f32[1,2,4,64]{3,2,1,0:T(4,128)S(1)}, u32[]{:S(2)}, u32[]{:S(2)}) collective-permute-start(f32[1,2,4,64]{3,2,1,0:T(4,128)S(1)} %get-tuple-element.37), channel_id=1, source_target_pairs={{8,0},{16,8},{24,16},{0,24},{9,1},{17,9},{25,17},{1,25},{10,2},{18... | collective-permute-start | bytes 6152 | tf_op jit(solution)/shard_map/ppermute | solution.py:19
  331.1 6.3 %collective-permute-start.40 = (f32[1,1,4,64]{3,2,1,0:T(4,128)S(1)}, f32[1,1,4,64]{3,2,1,0:T(4,128)S(1)}, u32[]{:S(2)}, u32[]{:S(2)}) collective-permute-start(f32[1,1,4,64]{3,2,1,0:T(4,128)S(1)} %get-tuple-element.39), channel_id=1, source_target_pairs={{0,1},{1,2},{2,3},{3,4},{4,5},{5,6},{6,7},{7,0},{8,9},{9,10},{10,1... | collective-permute-start | bytes 3080 | tf_op jit(solution)/shard_map/ppermute | solution.py:17
  333.3 4.0 collective-permute-start.41
  347.4 6.5 %collective-permute-start.46 = (f32[1,2,4,64]{3,2,1,0:T(4,128)S(1)}, f32[1,2,4,64]{3,2,1,0:T(4,128)S(1)}, u32[]{:S(2)}, u32[]{:S(2)}) collective-permute-start(f32[1,2,4,64]{3,2,1,0:T(4,128)S(1)} %get-tuple-element.33), channel_id=1, source_target_pairs={{0,8},{8,16},{16,24},{24,0},{1,9},{9,17},{17,25},{25,1},{2,10},{10... | collective-permute-start | bytes 6152 | tf_op jit(solution)/shard_map/ppermute | solution.py:17
  347.4 8.0 %collective-permute-start.47 = (f32[1,2,4,64]{3,2,1,0:T(4,128)S(1)}, f32[1,2,4,64]{3,2,1,0:T(4,128)S(1)}, u32[]{:S(2)}, u32[]{:S(2)}) collective-permute-start(f32[1,2,4,64]{3,2,1,0:T(4,128)S(1)} %get-tuple-element.33), channel_id=1, source_target_pairs={{8,0},{16,8},{24,16},{0,24},{9,1},{17,9},{25,17},{1,25},{10,2},{18... | collective-permute-start | bytes 6152 | tf_op jit(solution)/shard_map/ppermute | solution.py:19
  349.2 6.3 %collective-permute-start.44 = (f32[1,1,4,64]{3,2,1,0:T(4,128)S(1)}, f32[1,1,4,64]{3,2,1,0:T(4,128)S(1)}, u32[]{:S(2)}, u32[]{:S(2)}) collective-permute-start(f32[1,1,4,64]{3,2,1,0:T(4,128)S(1)} %get-tuple-element.35), channel_id=1, source_target_pairs={{0,1},{1,2},{2,3},{3,4},{4,5},{5,6},{6,7},{7,0},{8,9},{9,10},{10,1... | collective-permute-start | bytes 3080 | tf_op jit(solution)/shard_map/ppermute | solution.py:17
  351.0 4.5 collective-permute-start.45
  365.2 6.5 %collective-permute-start.50 = (f32[1,2,4,64]{3,2,1,0:T(4,128)S(1)}, f32[1,2,4,64]{3,2,1,0:T(4,128)S(1)}, u32[]{:S(2)}, u32[]{:S(2)}) collective-permute-start(f32[1,2,4,64]{3,2,1,0:T(4,128)S(1)} %get-tuple-element.29), channel_id=1, source_target_pairs={{0,8},{8,16},{16,24},{24,0},{1,9},{9,17},{17,25},{25,1},{2,10},{10... | collective-permute-start | bytes 6152 | tf_op jit(solution)/shard_map/ppermute | solution.py:17
  365.3 8.0 %collective-permute-start.51 = (f32[1,2,4,64]{3,2,1,0:T(4,128)S(1)}, f32[1,2,4,64]{3,2,1,0:T(4,128)S(1)}, u32[]{:S(2)}, u32[]{:S(2)}) collective-permute-start(f32[1,2,4,64]{3,2,1,0:T(4,128)S(1)} %get-tuple-element.29), channel_id=1, source_target_pairs={{8,0},{16,8},{24,16},{0,24},{9,1},{17,9},{25,17},{1,25},{10,2},{18... | collective-permute-start | bytes 6152 | tf_op jit(solution)/shard_map/ppermute | solution.py:19
  367.0 6.3 %collective-permute-start.48 = (f32[1,1,4,64]{3,2,1,0:T(4,128)S(1)}, f32[1,1,4,64]{3,2,1,0:T(4,128)S(1)}, u32[]{:S(2)}, u32[]{:S(2)}) collective-permute-start(f32[1,1,4,64]{3,2,1,0:T(4,128)S(1)} %get-tuple-element.31), channel_id=1, source_target_pairs={{0,1},{1,2},{2,3},{3,4},{4,5},{5,6},{6,7},{7,0},{8,9},{9,10},{10,1... | collective-permute-start | bytes 3080 | tf_op jit(solution)/shard_map/ppermute | solution.py:17
  368.4 4.9 %collective-permute-start.49 = (f32[1,1,4,64]{3,2,1,0:T(4,128)S(1)}, f32[1,1,4,64]{3,2,1,0:T(4,128)S(1)}, u32[]{:S(2)}, u32[]{:S(2)}) collective-permute-start(f32[1,1,4,64]{3,2,1,0:T(4,128)S(1)} %get-tuple-element.32), channel_id=1, source_target_pairs={{1,0},{2,1},{3,2},{4,3},{5,4},{6,5},{7,6},{0,7},{9,8},{10,9},{11,1... | collective-permute-start | bytes 3080 | tf_op jit(solution)/shard_map/ppermute | solution.py:19
  404.6 6.5 %collective-permute-start.54 = (f32[1,2,4,64]{3,2,1,0:T(4,128)S(1)}, f32[1,2,4,64]{3,2,1,0:T(4,128)S(1)}, u32[]{:S(2)}, u32[]{:S(2)}) collective-permute-start(f32[1,2,4,64]{3,2,1,0:T(4,128)S(1)} %get-tuple-element.25), channel_id=1, source_target_pairs={{0,8},{8,16},{16,24},{24,0},{1,9},{9,17},{17,25},{25,1},{2,10},{10... | collective-permute-start | bytes 6152 | tf_op jit(solution)/shard_map/ppermute | solution.py:17
  404.7 8.0 %collective-permute-start.55 = (f32[1,2,4,64]{3,2,1,0:T(4,128)S(1)}, f32[1,2,4,64]{3,2,1,0:T(4,128)S(1)}, u32[]{:S(2)}, u32[]{:S(2)}) collective-permute-start(f32[1,2,4,64]{3,2,1,0:T(4,128)S(1)} %get-tuple-element.25), channel_id=1, source_target_pairs={{8,0},{16,8},{24,16},{0,24},{9,1},{17,9},{25,17},{1,25},{10,2},{18... | collective-permute-start | bytes 6152 | tf_op jit(solution)/shard_map/ppermute | solution.py:19
  406.4 6.3 %collective-permute-start.52 = (f32[1,1,4,64]{3,2,1,0:T(4,128)S(1)}, f32[1,1,4,64]{3,2,1,0:T(4,128)S(1)}, u32[]{:S(2)}, u32[]{:S(2)}) collective-permute-start(f32[1,1,4,64]{3,2,1,0:T(4,128)S(1)} %get-tuple-element.27), channel_id=1, source_target_pairs={{0,1},{1,2},{2,3},{3,4},{4,5},{5,6},{6,7},{7,0},{8,9},{9,10},{10,1... | collective-permute-start | bytes 3080 | tf_op jit(solution)/shard_map/ppermute | solution.py:17
  406.4 6.3 %collective-permute-start.53 = (f32[1,1,4,64]{3,2,1,0:T(4,128)S(1)}, f32[1,1,4,64]{3,2,1,0:T(4,128)S(1)}, u32[]{:S(2)}, u32[]{:S(2)}) collective-permute-start(f32[1,1,4,64]{3,2,1,0:T(4,128)S(1)} %get-tuple-element.28), channel_id=1, source_target_pairs={{1,0},{2,1},{3,2},{4,3},{5,4},{6,5},{7,6},{0,7},{9,8},{10,9},{11,1... | collective-permute-start | bytes 3080 | tf_op jit(solution)/shard_map/ppermute | solution.py:19
where the time goes:
time: 465 us; the launch traced here: 464 us
  blocking collectives  206 us (44%)
  local copies, waits for them, and re-layouts  139 us (30%)
  starting transfers between devices  92 us (20%)
  waiting for transfers between devices  20.7 us (4%)
    gather x14, local copies, waits for them, and re-layouts, jump(): picked = jnp.take_along_axis(facing, position, axis=-1)  134 us
    psum x3, blocking collectives, global_sums(): return lax.psum((first_dot, second_dot), ('srow', 'scol'))  122 us
    all_gather x4, blocking collectives, apply_inverse(): lax.all_gather(coarse_in, 'scol', axis=0, tiled=True)  84.1 us
    ppermute x28, starting transfers between devices, with_halo(): lax.ppermute(head, axis, [((i + 1) % count, i) for i in range(count)])  78.3 us
    ppermute x28, waiting for transfers between devices, with_halo(): lax.ppermute(tail, axis, [(i, (i + 1) % count) for i in range(count)])  20.7 us
    ppermute x28, starting transfers between devices, with_halo(): lax.ppermute(tail, axis, [(i, (i + 1) % count) for i in range(count)])  13.7 us
  transfers between devices with their start and end apart: 56, of which 14 were waited for; matrix products, arithmetic and copies ran while one was open for 0% of the time, Pallas kernels for 0%

commit v1 on v0

--- a/solution.py
+++ b/solution.py
@@ -50,11 +50,32 @@
     coarse_in = jnp.einsum("ijb,ijrb->ijr", corner_coupling, values, precision=precise)
     coarse_in = coarse_in.reshape(sub_rows * sub_cols, rhs_count)
     band_rows = coarse_inverse[0]
+
+    def settle_tables(raw):
+        frame_out, y, block_next = (lax.axis_size("scol"), lax.axis_index("scol"), raw.shape[0])
+        view_out, state_next = (raw, 1)
+        while state_next < frame_out:
+            view_out = jnp.concatenate(
+                [
+                    view_out,
+                    lax.ppermute(
+                        view_out,
+                        "scol",
+                        list(
+                            map(
+                                lambda hop_no: (hop_no, (hop_no - state_next) % frame_out),
+                                range(frame_out),
+                            )
+                        ),
+                    ),
+                ],
+                axis=0,
+            )
+            state_next = 2 * state_next
+        return jnp.roll(view_out, shift=y * block_next, axis=0)
+
     coarse_out = jnp.dot(
-        band_rows,
-        lax.all_gather(coarse_in, "scol", axis=0, tiled=True),
-        precision=precise,
-        preferred_element_type=jnp.float32,
+        band_rows, settle_tables(coarse_in), precision=precise, preferred_element_type=jnp.float32
     )
     coarse_out = coarse_out.reshape(sub_rows, sub_cols, rhs_count)
     return blocks + corner_coupling[:, :, None, :] * coarse_out[..., None]

time: 465 us -> 446 us (0.959)
  blocking collectives: 206 us -> 122 us
  waiting for transfers between devices: 20.7 us -> 54.7 us
  starting transfers between devices: 92 us -> 123 us
    all_gather x4 -> x0, blocking collectives: 84.1 us -> none  [apply_inverse(): lax.all_gather(coarse_in, 'scol', axis=0, tiled=True)]
    ppermute x0 -> x12, waiting for transfers between devices: none -> 34 us  [settle_tables(): lax.ppermute(view_out, 'scol', list(map(lambda hop_no: (hop_no, (hop_no -...]
    ppermute x0 -> x12, starting transfers between devices: none -> 22.5 us  [settle_tables(): lax.ppermute(view_out, 'scol', list(map(lambda hop_no: (hop_no, (hop_no -...]
    ppermute x28, starting transfers between devices: 13.7 us -> 26.9 us  [with_halo(): lax.ppermute(tail, axis, [(i, (i + 1) % count) for i in range(count)])]
    ppermute x28, starting transfers between devices: 78.3 us -> 73.5 us  [with_halo(): lax.ppermute(head, axis, [((i + 1) % count, i) for i in range(count)])]
  transfers between devices with their start and end apart: 56 -> 68, of which waited for: 14 -> 26; matrix products, arithmetic and copies ran while one was open for 0% -> 0% of each run, Pallas kernels for 0% -> 0%
where the time goes in v1:
time: 446 us
  local copies, waits for them, and re-layouts  138 us (31%)
  starting transfers between devices  123 us (28%)
  blocking collectives  122 us (27%)
  waiting for transfers between devices  54.7 us (12%)
    gather x14, local copies, waits for them, and re-layouts, jump(): picked = jnp.take_along_axis(facing, position, axis=-1)  134 us
    psum x3, blocking collectives, global_sums(): return lax.psum((first_dot, second_dot), ('srow', 'scol'))  122 us
    ppermute x28, starting transfers between devices, with_halo(): lax.ppermute(head, axis, [((i + 1) % count, i) for i in range(count)])  73.5 us
    ppermute x12, waiting for transfers between devices, settle_tables(): lax.ppermute(view_out, 'scol', list(map(lambda hop_no: (hop_no, (hop_no -...  34 us
    ppermute x28, starting transfers between devices, with_halo(): lax.ppermute(tail, axis, [(i, (i + 1) % count) for i in range(count)])  26.9 us
    ppermute x12, starting transfers between devices, settle_tables(): lax.ppermute(view_out, 'scol', list(map(lambda hop_no: (hop_no, (hop_no -...  22.5 us
    ppermute x28, waiting for transfers between devices, with_halo(): lax.ppermute(tail, axis, [(i, (i + 1) % count) for i in range(count)])  20.6 us
  transfers between devices with their start and end apart: 68, of which 26 were waited for; matrix products, arithmetic and copies ran while one was open for 0% of the time, Pallas kernels for 0%

profile of v1, /device:TPU:0, one launch (start us, length us, event | category | flops | bytes accessed | tf_op | source)
XLA Modules:
  0.0 445.8 jit_solution(7945618859425316530)
XLA Ops:
  2.0 1.9 collective-permute-start.3
  4.0 2.3 collective-permute-start
  6.2 3.1 collective-permute-start.1
  10.9 9.6 %gather_fusion = f32[1024]{0:T(1024)S(1)} fusion(f32[2,4,128]{2,1,0:T(4,128)S(1)} %fusion.69, s32[1024]{0:T(1024)S(1)} %bitcast.180), kind=kCustom, calls=%fused_computation.clone | custom fusion | bytes 20480 | tf_op jit(solution)/shard_map/jit(take_along_axis)/gather | solution.py:43
  21.4 4.8 %collective-permute-start.4 = (f32[2,4]{0,1:T(4,128)S(1)}, f32[2,4]{0,1:T(4,128)S(1)}, u32[]{:S(2)}, u32[]{:S(2)}) collective-permute-start(f32[2,4]{0,1:T(4,128)S(1)} %bitcast.198), channel_id=1, source_target_pairs={{0,7},{1,0},{2,1},{3,2},{4,3},{5,4},{6,5},{7,6},{8,15},{9,8},{10,9... | collective-permute-start | bytes 104 | tf_op jit(solution)/shard_map/ppermute | solution.py:61
  28.4 2.8 collective-permute-done.5
  31.3 4.4 collective-permute-done.6
  36.5 1.7 collective-permute-start.10
  38.2 3.3 collective-permute-start.7
  41.5 3.5 collective-permute-start.8
  46.6 9.6 %gather_fusion.1 = f32[1024]{0:T(1024)S(1)} fusion(f32[2,4,128]{2,1,0:T(4,128)S(1)} %fusion.65, s32[1024]{0:T(1024)S(1)} %bitcast.181), kind=kCustom, calls=%fused_computation.1.clone | custom fusion | bytes 20480 | tf_op jit(solution)/shard_map/jit(take_along_axis)/gather | solution.py:43
  56.3 1.7 collective-permute-start.14
  58.1 4.7 %collective-permute-start.12 = (f32[1,1,4,64]{3,2,1,0:T(4,128)S(1)}, f32[1,1,4,64]{3,2,1,0:T(4,128)S(1)}, u32[]{:S(2)}, u32[]{:S(2)}) collective-permute-start(f32[1,1,4,64]{3,2,1,0:T(4,128)S(1)} %get-tuple-element.73), channel_id=1, source_target_pairs={{1,0},{2,1},{3,2},{4,3},{5,4},{6,5},{7,6},{0,7},{9,8},{10,9},{11,1... | collective-permute-start | bytes 3080 | tf_op jit(solution)/shard_map/ppermute | solution.py:19
  64.5 9.6 %gather_fusion.2 = f32[1024]{0:T(1024)S(1)} fusion(f32[2,4,128]{2,1,0:T(4,128)S(1)} %fusion.61, s32[1024]{0:T(1024)S(1)} %bitcast.182), kind=kCustom, calls=%fused_computation.2.clone | custom fusion | bytes 20480 | tf_op jit(solution)/shard_map/jit(take_along_axis)/gather | solution.py:43
  74.5 1.8 collective-permute-start.18
  76.2 4.7 %collective-permute-start.16 = (f32[1,1,4,64]{3,2,1,0:T(4,128)S(1)}, f32[1,1,4,64]{3,2,1,0:T(4,128)S(1)}, u32[]{:S(2)}, u32[]{:S(2)}) collective-permute-start(f32[1,1,4,64]{3,2,1,0:T(4,128)S(1)} %get-tuple-element.69), channel_id=1, source_target_pairs={{1,0},{2,1},{3,2},{4,3},{5,4},{6,5},{7,6},{0,7},{9,8},{10,9},{11,1... | collective-permute-start | bytes 3080 | tf_op jit(solution)/shard_map/ppermute | solution.py:19
  82.6 9.6 %gather_fusion.3 = f32[1024]{0:T(1024)S(1)} fusion(f32[2,4,128]{2,1,0:T(4,128)S(1)} %fusion.57, s32[1024]{0:T(1024)S(1)} %bitcast.183), kind=kCustom, calls=%fused_computation.3.clone | custom fusion | bytes 20480 | tf_op jit(solution)/shard_map/jit(take_along_axis)/gather | solution.py:43
  92.3 1.7 collective-permute-start.22
  94.1 4.7 %collective-permute-start.20 = (f32[1,1,4,64]{3,2,1,0:T(4,128)S(1)}, f32[1,1,4,64]{3,2,1,0:T(4,128)S(1)}, u32[]{:S(2)}, u32[]{:S(2)}) collective-permute-start(f32[1,1,4,64]{3,2,1,0:T(4,128)S(1)} %get-tuple-element.65), channel_id=1, source_target_pairs={{1,0},{2,1},{3,2},{4,3},{5,4},{6,5},{7,6},{0,7},{9,8},{10,9},{11,1... | collective-permute-start | bytes 3080 | tf_op jit(solution)/shard_map/ppermute | solution.py:19
  100.4 9.6 %gather_fusion.4 = f32[1024]{0:T(1024)S(1)} fusion(f32[2,4,128]{2,1,0:T(4,128)S(1)} %fusion.53, s32[1024]{0:T(1024)S(1)} %bitcast.184), kind=kCustom, calls=%fused_computation.4.clone | custom fusion | bytes 20480 | tf_op jit(solution)/shard_map/jit(take_along_axis)/gather | solution.py:43
  110.3 4.7 %collective-permute-start.23 = (f32[2,4]{0,1:T(4,128)S(1)}, f32[2,4]{0,1:T(4,128)S(1)}, u32[]{:S(2)}, u32[]{:S(2)}) collective-permute-start(f32[2,4]{0,1:T(4,128)S(1)} %bitcast.202), channel_id=1, source_target_pairs={{0,7},{1,0},{2,1},{3,2},{4,3},{5,4},{6,5},{7,6},{8,15},{9,8},{10,9... | collective-permute-start | bytes 104 | tf_op jit(solution)/shard_map/ppermute | solution.py:61
  117.2 2.8 collective-permute-done.24
  120.1 4.5 %collective-permute-done.25 = f32[8,4]{0,1:T(4,128)S(1)} collective-permute-done((f32[8,4]{0,1:T(4,128)S(1)}, f32[8,4]{0,1:T(4,128)S(1)}, u32[]{:S(2)}, u32[]{:S(2)}) %collective-permute-start.25) | collective-permute-done | bytes 160 | tf_op jit(solution)/shard_map/ppermute | solution.py:61
  125.2 1.7 collective-permute-start.29
  127.0 3.3 collective-permute-start.26
  130.2 3.5 collective-permute-start.27
  135.4 9.6 %gather_fusion.5 = f32[1024]{0:T(1024)S(1)} fusion(f32[2,4,128]{2,1,0:T(4,128)S(1)} %fusion.49, s32[1024]{0:T(1024)S(1)} %bitcast.185), kind=kCustom, calls=%fused_computation.5.clone | custom fusion | bytes 20480 | tf_op jit(solution)/shard_map/jit(take_along_axis)/gather | solution.py:43
  145.1 40.2 %all-reduce.2 = (f32[4]{0:T(128)S(1)}, f32[4]{0:T(128)S(1)}) all-reduce(f32[4]{0:T(128)S(1)} %get-tuple-element.9, f32[4]{0:T(128)S(1)} %get-tuple-element.8), channel_id=1, replica_groups=mesh['srow'=4,'scol'=8] {'srow','scol'}, use_global_device_ids=true, to_apply=%region_1.4 | all-reduce | flops 8 | bytes 64 | tf_op jit(solution)/shard_map/psum | solution.py:89
  185.5 1.7 collective-permute-start.33
  187.3 2.3 collective-permute-start.30
  189.6 2.4 collective-permute-start.31
  193.6 9.6 %gather_fusion.6 = f32[1024]{0:T(1024)S(1)} fusion(f32[2,4,128]{2,1,0:T(4,128)S(1)} %fusion.45, s32[1024]{0:T(1024)S(1)} %bitcast.186), kind=kCustom, calls=%fused_computation.6.clone | custom fusion | bytes 20480 | tf_op jit(solution)/shard_map/jit(take_along_axis)/gather | solution.py:43
  203.6 1.8 collective-permute-start.37
  205.4 1.8 collective-permute-start.34
  207.2 2.9 collective-permute-start.35
  211.8 9.6 %gather_fusion.7 = f32[1024]{0:T(1024)S(1)} fusion(f32[2,4,128]{2,1,0:T(4,128)S(1)} %fusion.41, s32[1024]{0:T(1024)S(1)} %bitcast.187), kind=kCustom, calls=%fused_computation.7.clone | custom fusion | bytes 20480 | tf_op jit(solution)/shard_map/jit(take_along_axis)/gather | solution.py:43
  224.6 3.4 collective-permute-start.39
  229.6 9.6 %gather_fusion.8 = f32[1024]{0:T(1024)S(1)} fusion(f32[2,4,128]{2,1,0:T(4,128)S(1)} %fusion.37, s32[1024]{0:T(1024)S(1)} %bitcast.188), kind=kCustom, calls=%fused_computation.8.clone | custom fusion | bytes 20480 | tf_op jit(solution)/shard_map/jit(take_along_axis)/gather | solution.py:43
  239.4 4.7 %collective-permute-start.42 = (f32[2,4]{0,1:T(4,128)S(1)}, f32[2,4]{0,1:T(4,128)S(1)}, u32[]{:S(2)}, u32[]{:S(2)}) collective-permute-start(f32[2,4]{0,1:T(4,128)S(1)} %bitcast.206), channel_id=1, source_target_pairs={{0,7},{1,0},{2,1},{3,2},{4,3},{5,4},{6,5},{7,6},{8,15},{9,8},{10,9... | collective-permute-start | bytes 104 | tf_op jit(solution)/shard_map/ppermute | solution.py:61
  246.5 2.6 collective-permute-done.43
  249.2 4.5 %collective-permute-done.44 = f32[8,4]{0,1:T(4,128)S(1)} collective-permute-done((f32[8,4]{0,1:T(4,128)S(1)}, f32[8,4]{0,1:T(4,128)S(1)}, u32[]{:S(2)}, u32[]{:S(2)}) %collective-permute-start.44) | collective-permute-done | bytes 160 | tf_op jit(solution)/shard_map/ppermute | solution.py:61
  254.4 1.7 collective-permute-start.48
  256.1 3.4 collective-permute-start.45
  259.6 3.5 collective-permute-start.46
  264.7 9.6 %gather_fusion.9 = f32[1024]{0:T(1024)S(1)} fusion(f32[2,4,128]{2,1,0:T(4,128)S(1)} %fusion.33, s32[1024]{0:T(1024)S(1)} %bitcast.189), kind=kCustom, calls=%fused_computation.9.clone | custom fusion | bytes 20480 | tf_op jit(solution)/shard_map/jit(take_along_axis)/gather | solution.py:43
  274.5 40.8 %all-reduce.1 = (f32[4]{0:T(128)S(1)}, f32[4]{0:T(128)S(1)}) all-reduce(f32[4]{0:T(128)S(1)} %get-tuple-element.7, f32[4]{0:T(128)S(1)} %get-tuple-element.6), channel_id=1, replica_groups=mesh['srow'=4,'scol'=8] {'srow','scol'}, use_global_device_ids=true, to_apply=%region_5.8 | all-reduce | flops 8 | bytes 64 | tf_op jit(solution)/shard_map/psum | solution.py:89
  315.5 1.8 collective-permute-start.52
  317.2 2.3 collective-permute-start.49
  319.5 2.4 collective-permute-start.50
  323.6 9.6 %gather_fusion.10 = f32[1024]{0:T(1024)S(1)} fusion(f32[2,4,128]{2,1,0:T(4,128)S(1)} %fusion.29, s32[1024]{0:T(1024)S(1)} %bitcast.190), kind=kCustom, calls=%fused_computation.10.clone | custom fusion | bytes 20480 | tf_op jit(solution)/shard_map/jit(take_along_axis)/gather | solution.py:43
  333.6 1.8 collective-permute-start.56
  335.4 1.8 collective-permute-start.53
  337.1 2.9 collective-permute-start.54
  341.7 9.6 %gather_fusion.11 = f32[1024]{0:T(1024)S(1)} fusion(f32[2,4,128]{2,1,0:T(4,128)S(1)} %fusion.25, s32[1024]{0:T(1024)S(1)} %bitcast.191), kind=kCustom, calls=%fused_computation.11.clone | custom fusion | bytes 20480 | tf_op jit(solution)/shard_map/jit(take_along_axis)/gather | solution.py:43
  354.5 3.4 collective-permute-start.58
  359.5 9.6 %gather_fusion.12 = f32[1024]{0:T(1024)S(1)} fusion(f32[2,4,128]{2,1,0:T(4,128)S(1)} %fusion.21, s32[1024]{0:T(1024)S(1)} %bitcast.192), kind=kCustom, calls=%fused_computation.12.clone | custom fusion | bytes 20480 | tf_op jit(solution)/shard_map/jit(take_along_axis)/gather | solution.py:43
  369.4 4.7 %collective-permute-start.61 = (f32[2,4]{0,1:T(4,128)S(1)}, f32[2,4]{0,1:T(4,128)S(1)}, u32[]{:S(2)}, u32[]{:S(2)}) collective-permute-start(f32[2,4]{0,1:T(4,128)S(1)} %bitcast.210), channel_id=1, source_target_pairs={{0,7},{1,0},{2,1},{3,2},{4,3},{5,4},{6,5},{7,6},{8,15},{9,8},{10,9... | collective-permute-start | bytes 104 | tf_op jit(solution)/shard_map/ppermute | solution.py:61
  376.3 2.8 collective-permute-done.62
  379.2 4.5 %collective-permute-done.63 = f32[8,4]{0,1:T(4,128)S(1)} collective-permute-done((f32[8,4]{0,1:T(4,128)S(1)}, f32[8,4]{0,1:T(4,128)S(1)}, u32[]{:S(2)}, u32[]{:S(2)}) %collective-permute-start.63) | collective-permute-done | bytes 160 | tf_op jit(solution)/shard_map/ppermute | solution.py:61
  384.3 1.7 collective-permute-start.67
  386.1 3.3 collective-permute-start.64
  389.4 3.5 collective-permute-start.65
  394.5 9.6 %gather_fusion.13 = f32[1024]{0:T(1024)S(1)} fusion(f32[2,4,128]{2,1,0:T(4,128)S(1)} %fusion.17, s32[1024]{0:T(1024)S(1)} %bitcast.193), kind=kCustom, calls=%fused_computation.13.clone | custom fusion | bytes 20480 | tf_op jit(solution)/shard_map/jit(take_along_axis)/gather | solution.py:43
  404.3 40.8 %all-reduce = (f32[4]{0:T(128)S(1)}, f32[4]{0:T(128)S(1)}) all-reduce(f32[4]{0:T(128)S(1)} %get-tuple-element.5, f32[4]{0:T(128)S(1)} %get-tuple-element.4), channel_id=1, replica_groups=mesh['srow'=4,'scol'=8] {'srow','scol'}, use_global_device_ids=true, to_apply=%region_9.12 | all-reduce | flops 8 | bytes 64 | tf_op jit(solution)/shard_map/psum | solution.py:89
  (207 shorter events, 47.0 us)
Async XLA Ops:
  1.5 7.9 %collective-permute-start.2 = (f32[1,2,4,64]{3,2,1,0:T(4,128)S(1)}, f32[1,2,4,64]{3,2,1,0:T(4,128)S(1)}, u32[]{:S(2)}, u32[]{:S(2)}) collective-permute-start(f32[1,2,4,64]{3,2,1,0:T(4,128)S(1)} %get-tuple-element.78), channel_id=1, source_target_pairs={{0,8},{8,16},{16,24},{24,0},{1,9},{9,17},{17,25},{25,1},{2,10},{10... | collective-permute-start | bytes 6152 | tf_op jit(solution)/shard_map/ppermute | solution.py:17
  2.0 8.8 %collective-permute-start.3 = (f32[1,2,4,64]{3,2,1,0:T(4,128)S(1)}, f32[1,2,4,64]{3,2,1,0:T(4,128)S(1)}, u32[]{:S(2)}, u32[]{:S(2)}) collective-permute-start(f32[1,2,4,64]{3,2,1,0:T(4,128)S(1)} %get-tuple-element.78), channel_id=1, source_target_pairs={{8,0},{16,8},{24,16},{0,24},{9,1},{17,9},{25,17},{1,25},{10,2},{18... | collective-permute-start | bytes 6152 | tf_op jit(solution)/shard_map/ppermute | solution.py:19
  4.0 6.9 %collective-permute-start = (f32[1,1,4,64]{3,2,1,0:T(4,128)S(1)}, f32[1,1,4,64]{3,2,1,0:T(4,128)S(1)}, u32[]{:S(2)}, u32[]{:S(2)}) collective-permute-start(f32[1,1,4,64]{3,2,1,0:T(4,128)S(1)} %get-tuple-element.80), channel_id=1, source_target_pairs={{0,1},{1,2},{2,3},{3,4},{4,5},{5,6},{6,7},{7,0},{8,9},{9,10},{10,1... | collective-permute-start | bytes 3080 | tf_op jit(solution)/shard_map/ppermute | solution.py:17
  6.2 4.6 %collective-permute-start.1 = (f32[1,1,4,64]{3,2,1,0:T(4,128)S(1)}, f32[1,1,4,64]{3,2,1,0:T(4,128)S(1)}, u32[]{:S(2)}, u32[]{:S(2)}) collective-permute-start(f32[1,1,4,64]{3,2,1,0:T(4,128)S(1)} %get-tuple-element.81), channel_id=1, source_target_pairs={{1,0},{2,1},{3,2},{4,3},{5,4},{6,5},{7,6},{0,7},{9,8},{10,9},{11,1... | collective-permute-start | bytes 3080 | tf_op jit(solution)/shard_map/ppermute | solution.py:19
  21.4 6.1 %collective-permute-start.4 = (f32[2,4]{0,1:T(4,128)S(1)}, f32[2,4]{0,1:T(4,128)S(1)}, u32[]{:S(2)}, u32[]{:S(2)}) collective-permute-start(f32[2,4]{0,1:T(4,128)S(1)} %bitcast.198), channel_id=1, source_target_pairs={{0,7},{1,0},{2,1},{3,2},{4,3},{5,4},{6,5},{7,6},{8,15},{9,8},{10,9... | collective-permute-start | bytes 104 | tf_op jit(solution)/shard_map/ppermute | solution.py:61
  31.3 4.5 %collective-permute-start.6 = (f32[8,4]{0,1:T(4,128)S(1)}, f32[8,4]{0,1:T(4,128)S(1)}, u32[]{:S(2)}, u32[]{:S(2)}) collective-permute-start(f32[8,4]{0,1:T(4,128)S(1)} %pad_maximum_fusion.15), channel_id=1, source_target_pairs={{0,4},{1,5},{2,6},{3,7},{4,0},{5,1},{6,2},{7,3},{8,12},{9,13},{10,... | collective-permute-start | bytes 392 | tf_op jit(solution)/shard_map/ppermute | solution.py:61
  36.4 8.5 %collective-permute-start.9 = (f32[1,2,4,64]{3,2,1,0:T(4,128)S(1)}, f32[1,2,4,64]{3,2,1,0:T(4,128)S(1)}, u32[]{:S(2)}, u32[]{:S(2)}) collective-permute-start(f32[1,2,4,64]{3,2,1,0:T(4,128)S(1)} %get-tuple-element.74), channel_id=1, source_target_pairs={{0,8},{8,16},{16,24},{24,0},{1,9},{9,17},{17,25},{25,1},{2,10},{10... | collective-permute-start | bytes 6152 | tf_op jit(solution)/shard_map/ppermute | solution.py:17
  36.5 10.1 %collective-permute-start.10 = (f32[1,2,4,64]{3,2,1,0:T(4,128)S(1)}, f32[1,2,4,64]{3,2,1,0:T(4,128)S(1)}, u32[]{:S(2)}, u32[]{:S(2)}) collective-permute-start(f32[1,2,4,64]{3,2,1,0:T(4,128)S(1)} %get-tuple-element.74), channel_id=1, source_target_pairs={{8,0},{16,8},{24,16},{0,24},{9,1},{17,9},{25,17},{1,25},{10,2},{18... | collective-permute-start | bytes 6152 | tf_op jit(solution)/shard_map/ppermute | solution.py:19
  38.2 8.3 %collective-permute-start.7 = (f32[1,1,4,64]{3,2,1,0:T(4,128)S(1)}, f32[1,1,4,64]{3,2,1,0:T(4,128)S(1)}, u32[]{:S(2)}, u32[]{:S(2)}) collective-permute-start(f32[1,1,4,64]{3,2,1,0:T(4,128)S(1)} %get-tuple-element.76), channel_id=1, source_target_pairs={{0,1},{1,2},{2,3},{3,4},{4,5},{5,6},{6,7},{7,0},{8,9},{9,10},{10,1... | collective-permute-start | bytes 3080 | tf_op jit(solution)/shard_map/ppermute | solution.py:17
  41.5 5.1 %collective-permute-start.8 = (f32[1,1,4,64]{3,2,1,0:T(4,128)S(1)}, f32[1,1,4,64]{3,2,1,0:T(4,128)S(1)}, u32[]{:S(2)}, u32[]{:S(2)}) collective-permute-start(f32[1,1,4,64]{3,2,1,0:T(4,128)S(1)} %get-tuple-element.77), channel_id=1, source_target_pairs={{1,0},{2,1},{3,2},{4,3},{5,4},{6,5},{7,6},{0,7},{9,8},{10,9},{11,1... | collective-permute-start | bytes 3080 | tf_op jit(solution)/shard_map/ppermute | solution.py:19
  56.3 6.5 %collective-permute-start.13 = (f32[1,2,4,64]{3,2,1,0:T(4,128)S(1)}, f32[1,2,4,64]{3,2,1,0:T(4,128)S(1)}, u32[]{:S(2)}, u32[]{:S(2)}) collective-permute-start(f32[1,2,4,64]{3,2,1,0:T(4,128)S(1)} %get-tuple-element.70), channel_id=1, source_target_pairs={{0,8},{8,16},{16,24},{24,0},{1,9},{9,17},{17,25},{25,1},{2,10},{10... | collective-permute-start | bytes 6152 | tf_op jit(solution)/shard_map/ppermute | solution.py:17
  56.3 8.0 %collective-permute-start.14 = (f32[1,2,4,64]{3,2,1,0:T(4,128)S(1)}, f32[1,2,4,64]{3,2,1,0:T(4,128)S(1)}, u32[]{:S(2)}, u32[]{:S(2)}) collective-permute-start(f32[1,2,4,64]{3,2,1,0:T(4,128)S(1)} %get-tuple-element.70), channel_id=1, source_target_pairs={{8,0},{16,8},{24,16},{0,24},{9,1},{17,9},{25,17},{1,25},{10,2},{18... | collective-permute-start | bytes 6152 | tf_op jit(solution)/shard_map/ppermute | solution.py:19
  58.1 6.3 %collective-permute-start.11 = (f32[1,1,4,64]{3,2,1,0:T(4,128)S(1)}, f32[1,1,4,64]{3,2,1,0:T(4,128)S(1)}, u32[]{:S(2)}, u32[]{:S(2)}) collective-permute-start(f32[1,1,4,64]{3,2,1,0:T(4,128)S(1)} %get-tuple-element.72), channel_id=1, source_target_pairs={{0,1},{1,2},{2,3},{3,4},{4,5},{5,6},{6,7},{7,0},{8,9},{9,10},{10,1... | collective-permute-start | bytes 3080 | tf_op jit(solution)/shard_map/ppermute | solution.py:17
  58.1 6.3 %collective-permute-start.12 = (f32[1,1,4,64]{3,2,1,0:T(4,128)S(1)}, f32[1,1,4,64]{3,2,1,0:T(4,128)S(1)}, u32[]{:S(2)}, u32[]{:S(2)}) collective-permute-start(f32[1,1,4,64]{3,2,1,0:T(4,128)S(1)} %get-tuple-element.73), channel_id=1, source_target_pairs={{1,0},{2,1},{3,2},{4,3},{5,4},{6,5},{7,6},{0,7},{9,8},{10,9},{11,1... | collective-permute-start | bytes 3080 | tf_op jit(solution)/shard_map/ppermute | solution.py:19
  74.5 6.5 %collective-permute-start.17 = (f32[1,2,4,64]{3,2,1,0:T(4,128)S(1)}, f32[1,2,4,64]{3,2,1,0:T(4,128)S(1)}, u32[]{:S(2)}, u32[]{:S(2)}) collective-permute-start(f32[1,2,4,64]{3,2,1,0:T(4,128)S(1)} %get-tuple-element.66), channel_id=1, source_target_pairs={{0,8},{8,16},{16,24},{24,0},{1,9},{9,17},{17,25},{25,1},{2,10},{10... | collective-permute-start | bytes 6152 | tf_op jit(solution)/shard_map/ppermute | solution.py:17
  74.5 8.0 %collective-permute-start.18 = (f32[1,2,4,64]{3,2,1,0:T(4,128)S(1)}, f32[1,2,4,64]{3,2,1,0:T(4,128)S(1)}, u32[]{:S(2)}, u32[]{:S(2)}) collective-permute-start(f32[1,2,4,64]{3,2,1,0:T(4,128)S(1)} %get-tuple-element.66), channel_id=1, source_target_pairs={{8,0},{16,8},{24,16},{0,24},{9,1},{17,9},{25,17},{1,25},{10,2},{18... | collective-permute-start | bytes 6152 | tf_op jit(solution)/shard_map/ppermute | solution.py:19
  76.2 6.3 %collective-permute-start.15 = (f32[1,1,4,64]{3,2,1,0:T(4,128)S(1)}, f32[1,1,4,64]{3,2,1,0:T(4,128)S(1)}, u32[]{:S(2)}, u32[]{:S(2)}) collective-permute-start(f32[1,1,4,64]{3,2,1,0:T(4,128)S(1)} %get-tuple-element.68), channel_id=1, source_target_pairs={{0,1},{1,2},{2,3},{3,4},{4,5},{5,6},{6,7},{7,0},{8,9},{9,10},{10,1... | collective-permute-start | bytes 3080 | tf_op jit(solution)/shard_map/ppermute | solution.py:17
  76.2 6.3 %collective-permute-start.16 = (f32[1,1,4,64]{3,2,1,0:T(4,128)S(1)}, f32[1,1,4,64]{3,2,1,0:T(4,128)S(1)}, u32[]{:S(2)}, u32[]{:S(2)}) collective-permute-start(f32[1,1,4,64]{3,2,1,0:T(4,128)S(1)} %get-tuple-element.69), channel_id=1, source_target_pairs={{1,0},{2,1},{3,2},{4,3},{5,4},{6,5},{7,6},{0,7},{9,8},{10,9},{11,1... | collective-permute-start | bytes 3080 | tf_op jit(solution)/shard_map/ppermute | solution.py:19
  92.3 6.5 %collective-permute-start.21 = (f32[1,2,4,64]{3,2,1,0:T(4,128)S(1)}, f32[1,2,4,64]{3,2,1,0:T(4,128)S(1)}, u32[]{:S(2)}, u32[]{:S(2)}) collective-permute-start(f32[1,2,4,64]{3,2,1,0:T(4,128)S(1)} %get-tuple-element.62), channel_id=1, source_target_pairs={{0,8},{8,16},{16,24},{24,0},{1,9},{9,17},{17,25},{25,1},{2,10},{10... | collective-permute-start | bytes 6152 | tf_op jit(solution)/shard_map/ppermute | solution.py:17
  92.3 8.0 %collective-permute-start.22 = (f32[1,2,4,64]{3,2,1,0:T(4,128)S(1)}, f32[1,2,4,64]{3,2,1,0:T(4,128)S(1)}, u32[]{:S(2)}, u32[]{:S(2)}) collective-permute-start(f32[1,2,4,64]{3,2,1,0:T(4,128)S(1)} %get-tuple-element.62), channel_id=1, source_target_pairs={{8,0},{16,8},{24,16},{0,24},{9,1},{17,9},{25,17},{1,25},{10,2},{18... | collective-permute-start | bytes 6152 | tf_op jit(solution)/shard_map/ppermute | solution.py:19
  94.0 6.3 %collective-permute-start.19 = (f32[1,1,4,64]{3,2,1,0:T(4,128)S(1)}, f32[1,1,4,64]{3,2,1,0:T(4,128)S(1)}, u32[]{:S(2)}, u32[]{:S(2)}) collective-permute-start(f32[1,1,4,64]{3,2,1,0:T(4,128)S(1)} %get-tuple-element.64), channel_id=1, source_target_pairs={{0,1},{1,2},{2,3},{3,4},{4,5},{5,6},{6,7},{7,0},{8,9},{9,10},{10,1... | collective-permute-start | bytes 3080 | tf_op jit(solution)/shard_map/ppermute | solution.py:17
  94.1 6.3 %collective-permute-start.20 = (f32[1,1,4,64]{3,2,1,0:T(4,128)S(1)}, f32[1,1,4,64]{3,2,1,0:T(4,128)S(1)}, u32[]{:S(2)}, u32[]{:S(2)}) collective-permute-start(f32[1,1,4,64]{3,2,1,0:T(4,128)S(1)} %get-tuple-element.65), channel_id=1, source_target_pairs={{1,0},{2,1},{3,2},{4,3},{5,4},{6,5},{7,6},{0,7},{9,8},{10,9},{11,1... | collective-permute-start | bytes 3080 | tf_op jit(solution)/shard_map/ppermute | solution.py:19
  110.3 6.0 %collective-permute-start.23 = (f32[2,4]{0,1:T(4,128)S(1)}, f32[2,4]{0,1:T(4,128)S(1)}, u32[]{:S(2)}, u32[]{:S(2)}) collective-permute-start(f32[2,4]{0,1:T(4,128)S(1)} %bitcast.202), channel_id=1, source_target_pairs={{0,7},{1,0},{2,1},{3,2},{4,3},{5,4},{6,5},{7,6},{8,15},{9,8},{10,9... | collective-permute-start | bytes 104 | tf_op jit(solution)/shard_map/ppermute | solution.py:61
  120.0 4.5 %collective-permute-start.25 = (f32[8,4]{0,1:T(4,128)S(1)}, f32[8,4]{0,1:T(4,128)S(1)}, u32[]{:S(2)}, u32[]{:S(2)}) collective-permute-start(f32[8,4]{0,1:T(4,128)S(1)} %pad_maximum_fusion.17), channel_id=1, source_target_pairs={{0,4},{1,5},{2,6},{3,7},{4,0},{5,1},{6,2},{7,3},{8,12},{9,13},{10,... | collective-permute-start | bytes 392 | tf_op jit(solution)/shard_map/ppermute | solution.py:61
  125.2 8.5 %collective-permute-start.28 = (f32[1,2,4,64]{3,2,1,0:T(4,128)S(1)}, f32[1,2,4,64]{3,2,1,0:T(4,128)S(1)}, u32[]{:S(2)}, u32[]{:S(2)}) collective-permute-start(f32[1,2,4,64]{3,2,1,0:T(4,128)S(1)} %get-tuple-element.58), channel_id=1, source_target_pairs={{0,8},{8,16},{16,24},{24,0},{1,9},{9,17},{17,25},{25,1},{2,10},{10... | collective-permute-start | bytes 6152 | tf_op jit(solution)/shard_map/ppermute | solution.py:17
  125.2 10.1 %collective-permute-start.29 = (f32[1,2,4,64]{3,2,1,0:T(4,128)S(1)}, f32[1,2,4,64]{3,2,1,0:T(4,128)S(1)}, u32[]{:S(2)}, u32[]{:S(2)}) collective-permute-start(f32[1,2,4,64]{3,2,1,0:T(4,128)S(1)} %get-tuple-element.58), channel_id=1, source_target_pairs={{8,0},{16,8},{24,16},{0,24},{9,1},{17,9},{25,17},{1,25},{10,2},{18... | collective-permute-start | bytes 6152 | tf_op jit(solution)/shard_map/ppermute | solution.py:19
  127.0 8.3 %collective-permute-start.26 = (f32[1,1,4,64]{3,2,1,0:T(4,128)S(1)}, f32[1,1,4,64]{3,2,1,0:T(4,128)S(1)}, u32[]{:S(2)}, u32[]{:S(2)}) collective-permute-start(f32[1,1,4,64]{3,2,1,0:T(4,128)S(1)} %get-tuple-element.60), channel_id=1, source_target_pairs={{0,1},{1,2},{2,3},{3,4},{4,5},{5,6},{6,7},{7,0},{8,9},{9,10},{10,1... | collective-permute-start | bytes 3080 | tf_op jit(solution)/shard_map/ppermute | solution.py:17
  130.2 5.1 %collective-permute-start.27 = (f32[1,1,4,64]{3,2,1,0:T(4,128)S(1)}, f32[1,1,4,64]{3,2,1,0:T(4,128)S(1)}, u32[]{:S(2)}, u32[]{:S(2)}) collective-permute-start(f32[1,1,4,64]{3,2,1,0:T(4,128)S(1)} %get-tuple-element.61), channel_id=1, source_target_pairs={{1,0},{2,1},{3,2},{4,3},{5,4},{6,5},{7,6},{0,7},{9,8},{10,9},{11,1... | collective-permute-start | bytes 3080 | tf_op jit(solution)/shard_map/ppermute | solution.py:19
  185.5 6.5 %collective-permute-start.32 = (f32[1,2,4,64]{3,2,1,0:T(4,128)S(1)}, f32[1,2,4,64]{3,2,1,0:T(4,128)S(1)}, u32[]{:S(2)}, u32[]{:S(2)}) collective-permute-start(f32[1,2,4,64]{3,2,1,0:T(4,128)S(1)} %get-tuple-element.54), channel_id=1, source_target_pairs={{0,8},{8,16},{16,24},{24,0},{1,9},{9,17},{17,25},{25,1},{2,10},{10... | collective-permute-start | bytes 6152 | tf_op jit(solution)/shard_map/ppermute | solution.py:17
  185.5 8.0 %collective-permute-start.33 = (f32[1,2,4,64]{3,2,1,0:T(4,128)S(1)}, f32[1,2,4,64]{3,2,1,0:T(4,128)S(1)}, u32[]{:S(2)}, u32[]{:S(2)}) collective-permute-start(f32[1,2,4,64]{3,2,1,0:T(4,128)S(1)} %get-tuple-element.54), channel_id=1, source_target_pairs={{8,0},{16,8},{24,16},{0,24},{9,1},{17,9},{25,17},{1,25},{10,2},{18... | collective-permute-start | bytes 6152 | tf_op jit(solution)/shard_map/ppermute | solution.py:19
  187.3 6.3 %collective-permute-start.30 = (f32[1,1,4,64]{3,2,1,0:T(4,128)S(1)}, f32[1,1,4,64]{3,2,1,0:T(4,128)S(1)}, u32[]{:S(2)}, u32[]{:S(2)}) collective-permute-start(f32[1,1,4,64]{3,2,1,0:T(4,128)S(1)} %get-tuple-element.56), channel_id=1, source_target_pairs={{0,1},{1,2},{2,3},{3,4},{4,5},{5,6},{6,7},{7,0},{8,9},{9,10},{10,1... | collective-permute-start | bytes 3080 | tf_op jit(solution)/shard_map/ppermute | solution.py:17
  189.6 4.0 collective-permute-start.31
  203.6 6.5 %collective-permute-start.36 = (f32[1,2,4,64]{3,2,1,0:T(4,128)S(1)}, f32[1,2,4,64]{3,2,1,0:T(4,128)S(1)}, u32[]{:S(2)}, u32[]{:S(2)}) collective-permute-start(f32[1,2,4,64]{3,2,1,0:T(4,128)S(1)} %get-tuple-element.50), channel_id=1, source_target_pairs={{0,8},{8,16},{16,24},{24,0},{1,9},{9,17},{17,25},{25,1},{2,10},{10... | collective-permute-start | bytes 6152 | tf_op jit(solution)/shard_map/ppermute | solution.py:17
  203.6 8.0 %collective-permute-start.37 = (f32[1,2,4,64]{3,2,1,0:T(4,128)S(1)}, f32[1,2,4,64]{3,2,1,0:T(4,128)S(1)}, u32[]{:S(2)}, u32[]{:S(2)}) collective-permute-start(f32[1,2,4,64]{3,2,1,0:T(4,128)S(1)} %get-tuple-element.50), channel_id=1, source_target_pairs={{8,0},{16,8},{24,16},{0,24},{9,1},{17,9},{25,17},{1,25},{10,2},{18... | collective-permute-start | bytes 6152 | tf_op jit(solution)/shard_map/ppermute | solution.py:19
  205.4 6.3 %collective-permute-start.34 = (f32[1,1,4,64]{3,2,1,0:T(4,128)S(1)}, f32[1,1,4,64]{3,2,1,0:T(4,128)S(1)}, u32[]{:S(2)}, u32[]{:S(2)}) collective-permute-start(f32[1,1,4,64]{3,2,1,0:T(4,128)S(1)} %get-tuple-element.52), channel_id=1, source_target_pairs={{0,1},{1,2},{2,3},{3,4},{4,5},{5,6},{6,7},{7,0},{8,9},{9,10},{10,1... | collective-permute-start | bytes 3080 | tf_op jit(solution)/shard_map/ppermute | solution.py:17
  207.2 4.5 %collective-permute-start.35 = (f32[1,1,4,64]{3,2,1,0:T(4,128)S(1)}, f32[1,1,4,64]{3,2,1,0:T(4,128)S(1)}, u32[]{:S(2)}, u32[]{:S(2)}) collective-permute-start(f32[1,1,4,64]{3,2,1,0:T(4,128)S(1)} %get-tuple-element.53), channel_id=1, source_target_pairs={{1,0},{2,1},{3,2},{4,3},{5,4},{6,5},{7,6},{0,7},{9,8},{10,9},{11,1... | collective-permute-start | bytes 3080 | tf_op jit(solution)/shard_map/ppermute | solution.py:19
  221.5 6.5 %collective-permute-start.40 = (f32[1,2,4,64]{3,2,1,0:T(4,128)S(1)}, f32[1,2,4,64]{3,2,1,0:T(4,128)S(1)}, u32[]{:S(2)}, u32[]{:S(2)}) collective-permute-start(f32[1,2,4,64]{3,2,1,0:T(4,128)S(1)} %get-tuple-element.46), channel_id=1, source_target_pairs={{0,8},{8,16},{16,24},{24,0},{1,9},{9,17},{17,25},{25,1},{2,10},{10... | collective-permute-start | bytes 6152 | tf_op jit(solution)/shard_map/ppermute | solution.py:17
  221.5 8.0 %collective-permute-start.41 = (f32[1,2,4,64]{3,2,1,0:T(4,128)S(1)}, f32[1,2,4,64]{3,2,1,0:T(4,128)S(1)}, u32[]{:S(2)}, u32[]{:S(2)}) collective-permute-start(f32[1,2,4,64]{3,2,1,0:T(4,128)S(1)} %get-tuple-element.46), channel_id=1, source_target_pairs={{8,0},{16,8},{24,16},{0,24},{9,1},{17,9},{25,17},{1,25},{10,2},{18... | collective-permute-start | bytes 6152 | tf_op jit(solution)/shard_map/ppermute | solution.py:19
  223.2 6.3 %collective-permute-start.38 = (f32[1,1,4,64]{3,2,1,0:T(4,128)S(1)}, f32[1,1,4,64]{3,2,1,0:T(4,128)S(1)}, u32[]{:S(2)}, u32[]{:S(2)}) collective-permute-start(f32[1,1,4,64]{3,2,1,0:T(4,128)S(1)} %get-tuple-element.48), channel_id=1, source_target_pairs={{0,1},{1,2},{2,3},{3,4},{4,5},{5,6},{6,7},{7,0},{8,9},{9,10},{10,1... | collective-permute-start | bytes 3080 | tf_op jit(solution)/shard_map/ppermute | solution.py:17
  224.6 4.9 %collective-permute-start.39 = (f32[1,1,4,64]{3,2,1,0:T(4,128)S(1)}, f32[1,1,4,64]{3,2,1,0:T(4,128)S(1)}, u32[]{:S(2)}, u32[]{:S(2)}) collective-permute-start(f32[1,1,4,64]{3,2,1,0:T(4,128)S(1)} %get-tuple-element.49), channel_id=1, source_target_pairs={{1,0},{2,1},{3,2},{4,3},{5,4},{6,5},{7,6},{0,7},{9,8},{10,9},{11,1... | collective-permute-start | bytes 3080 | tf_op jit(solution)/shard_map/ppermute | solution.py:19
  239.4 6.0 %collective-permute-start.42 = (f32[2,4]{0,1:T(4,128)S(1)}, f32[2,4]{0,1:T(4,128)S(1)}, u32[]{:S(2)}, u32[]{:S(2)}) collective-permute-start(f32[2,4]{0,1:T(4,128)S(1)} %bitcast.206), channel_id=1, source_target_pairs={{0,7},{1,0},{2,1},{3,2},{4,3},{5,4},{6,5},{7,6},{8,15},{9,8},{10,9... | collective-permute-start | bytes 104 | tf_op jit(solution)/shard_map/ppermute | solution.py:61
  249.2 4.5 %collective-permute-start.44 = (f32[8,4]{0,1:T(4,128)S(1)}, f32[8,4]{0,1:T(4,128)S(1)}, u32[]{:S(2)}, u32[]{:S(2)}) collective-permute-start(f32[8,4]{0,1:T(4,128)S(1)} %pad_maximum_fusion.19), channel_id=1, source_target_pairs={{0,4},{1,5},{2,6},{3,7},{4,0},{5,1},{6,2},{7,3},{8,12},{9,13},{10,... | collective-permute-start | bytes 392 | tf_op jit(solution)/shard_map/ppermute | solution.py:61
  254.4 8.7 %collective-permute-start.47 = (f32[1,2,4,64]{3,2,1,0:T(4,128)S(1)}, f32[1,2,4,64]{3,2,1,0:T(4,128)S(1)}, u32[]{:S(2)}, u32[]{:S(2)}) collective-permute-start(f32[1,2,4,64]{3,2,1,0:T(4,128)S(1)} %get-tuple-element.42), channel_id=1, source_target_pairs={{0,8},{8,16},{16,24},{24,0},{1,9},{9,17},{17,25},{25,1},{2,10},{10... | collective-permute-start | bytes 6152 | tf_op jit(solution)/shard_map/ppermute | solution.py:17
  254.4 10.2 %collective-permute-start.48 = (f32[1,2,4,64]{3,2,1,0:T(4,128)S(1)}, f32[1,2,4,64]{3,2,1,0:T(4,128)S(1)}, u32[]{:S(2)}, u32[]{:S(2)}) collective-permute-start(f32[1,2,4,64]{3,2,1,0:T(4,128)S(1)} %get-tuple-element.42), channel_id=1, source_target_pairs={{8,0},{16,8},{24,16},{0,24},{9,1},{17,9},{25,17},{1,25},{10,2},{18... | collective-permute-start | bytes 6152 | tf_op jit(solution)/shard_map/ppermute | solution.py:19
  256.1 8.5 %collective-permute-start.45 = (f32[1,1,4,64]{3,2,1,0:T(4,128)S(1)}, f32[1,1,4,64]{3,2,1,0:T(4,128)S(1)}, u32[]{:S(2)}, u32[]{:S(2)}) collective-permute-start(f32[1,1,4,64]{3,2,1,0:T(4,128)S(1)} %get-tuple-element.44), channel_id=1, source_target_pairs={{0,1},{1,2},{2,3},{3,4},{4,5},{5,6},{6,7},{7,0},{8,9},{9,10},{10,1... | collective-permute-start | bytes 3080 | tf_op jit(solution)/shard_map/ppermute | solution.py:17
  259.6 5.1 %collective-permute-start.46 = (f32[1,1,4,64]{3,2,1,0:T(4,128)S(1)}, f32[1,1,4,64]{3,2,1,0:T(4,128)S(1)}, u32[]{:S(2)}, u32[]{:S(2)}) collective-permute-start(f32[1,1,4,64]{3,2,1,0:T(4,128)S(1)} %get-tuple-element.45), channel_id=1, source_target_pairs={{1,0},{2,1},{3,2},{4,3},{5,4},{6,5},{7,6},{0,7},{9,8},{10,9},{11,1... | collective-permute-start | bytes 3080 | tf_op jit(solution)/shard_map/ppermute | solution.py:19
  315.5 6.5 %collective-permute-start.51 = (f32[1,2,4,64]{3,2,1,0:T(4,128)S(1)}, f32[1,2,4,64]{3,2,1,0:T(4,128)S(1)}, u32[]{:S(2)}, u32[]{:S(2)}) collective-permute-start(f32[1,2,4,64]{3,2,1,0:T(4,128)S(1)} %get-tuple-element.38), channel_id=1, source_target_pairs={{0,8},{8,16},{16,24},{24,0},{1,9},{9,17},{17,25},{25,1},{2,10},{10... | collective-permute-start | bytes 6152 | tf_op jit(solution)/shard_map/ppermute | solution.py:17
  315.5 8.0 %collective-permute-start.52 = (f32[1,2,4,64]{3,2,1,0:T(4,128)S(1)}, f32[1,2,4,64]{3,2,1,0:T(4,128)S(1)}, u32[]{:S(2)}, u32[]{:S(2)}) collective-permute-start(f32[1,2,4,64]{3,2,1,0:T(4,128)S(1)} %get-tuple-element.38), channel_id=1, source_target_pairs={{8,0},{16,8},{24,16},{0,24},{9,1},{17,9},{25,17},{1,25},{10,2},{18... | collective-permute-start | bytes 6152 | tf_op jit(solution)/shard_map/ppermute | solution.py:19
  317.2 6.3 %collective-permute-start.49 = (f32[1,1,4,64]{3,2,1,0:T(4,128)S(1)}, f32[1,1,4,64]{3,2,1,0:T(4,128)S(1)}, u32[]{:S(2)}, u32[]{:S(2)}) collective-permute-start(f32[1,1,4,64]{3,2,1,0:T(4,128)S(1)} %get-tuple-element.40), channel_id=1, source_target_pairs={{0,1},{1,2},{2,3},{3,4},{4,5},{5,6},{6,7},{7,0},{8,9},{9,10},{10,1... | collective-permute-start | bytes 3080 | tf_op jit(solution)/shard_map/ppermute | solution.py:17
  319.5 4.0 collective-permute-start.50
  333.6 6.5 %collective-permute-start.55 = (f32[1,2,4,64]{3,2,1,0:T(4,128)S(1)}, f32[1,2,4,64]{3,2,1,0:T(4,128)S(1)}, u32[]{:S(2)}, u32[]{:S(2)}) collective-permute-start(f32[1,2,4,64]{3,2,1,0:T(4,128)S(1)} %get-tuple-element.34), channel_id=1, source_target_pairs={{0,8},{8,16},{16,24},{24,0},{1,9},{9,17},{17,25},{25,1},{2,10},{10... | collective-permute-start | bytes 6152 | tf_op jit(solution)/shard_map/ppermute | solution.py:17
  333.6 8.0 %collective-permute-start.56 = (f32[1,2,4,64]{3,2,1,0:T(4,128)S(1)}, f32[1,2,4,64]{3,2,1,0:T(4,128)S(1)}, u32[]{:S(2)}, u32[]{:S(2)}) collective-permute-start(f32[1,2,4,64]{3,2,1,0:T(4,128)S(1)} %get-tuple-element.34), channel_id=1, source_target_pairs={{8,0},{16,8},{24,16},{0,24},{9,1},{17,9},{25,17},{1,25},{10,2},{18... | collective-permute-start | bytes 6152 | tf_op jit(solution)/shard_map/ppermute | solution.py:19
  335.4 6.3 %collective-permute-start.53 = (f32[1,1,4,64]{3,2,1,0:T(4,128)S(1)}, f32[1,1,4,64]{3,2,1,0:T(4,128)S(1)}, u32[]{:S(2)}, u32[]{:S(2)}) collective-permute-start(f32[1,1,4,64]{3,2,1,0:T(4,128)S(1)} %get-tuple-element.36), channel_id=1, source_target_pairs={{0,1},{1,2},{2,3},{3,4},{4,5},{5,6},{6,7},{7,0},{8,9},{9,10},{10,1... | collective-permute-start | bytes 3080 | tf_op jit(solution)/shard_map/ppermute | solution.py:17
  337.1 4.5 %collective-permute-start.54 = (f32[1,1,4,64]{3,2,1,0:T(4,128)S(1)}, f32[1,1,4,64]{3,2,1,0:T(4,128)S(1)}, u32[]{:S(2)}, u32[]{:S(2)}) collective-permute-start(f32[1,1,4,64]{3,2,1,0:T(4,128)S(1)} %get-tuple-element.37), channel_id=1, source_target_pairs={{1,0},{2,1},{3,2},{4,3},{5,4},{6,5},{7,6},{0,7},{9,8},{10,9},{11,1... | collective-permute-start | bytes 3080 | tf_op jit(solution)/shard_map/ppermute | solution.py:19
  351.4 6.5 %collective-permute-start.59 = (f32[1,2,4,64]{3,2,1,0:T(4,128)S(1)}, f32[1,2,4,64]{3,2,1,0:T(4,128)S(1)}, u32[]{:S(2)}, u32[]{:S(2)}) collective-permute-start(f32[1,2,4,64]{3,2,1,0:T(4,128)S(1)} %get-tuple-element.30), channel_id=1, source_target_pairs={{0,8},{8,16},{16,24},{24,0},{1,9},{9,17},{17,25},{25,1},{2,10},{10... | collective-permute-start | bytes 6152 | tf_op jit(solution)/shard_map/ppermute | solution.py:17
  351.4 8.0 %collective-permute-start.60 = (f32[1,2,4,64]{3,2,1,0:T(4,128)S(1)}, f32[1,2,4,64]{3,2,1,0:T(4,128)S(1)}, u32[]{:S(2)}, u32[]{:S(2)}) collective-permute-start(f32[1,2,4,64]{3,2,1,0:T(4,128)S(1)} %get-tuple-element.30), channel_id=1, source_target_pairs={{8,0},{16,8},{24,16},{0,24},{9,1},{17,9},{25,17},{1,25},{10,2},{18... | collective-permute-start | bytes 6152 | tf_op jit(solution)/shard_map/ppermute | solution.py:19
  353.2 6.3 %collective-permute-start.57 = (f32[1,1,4,64]{3,2,1,0:T(4,128)S(1)}, f32[1,1,4,64]{3,2,1,0:T(4,128)S(1)}, u32[]{:S(2)}, u32[]{:S(2)}) collective-permute-start(f32[1,1,4,64]{3,2,1,0:T(4,128)S(1)} %get-tuple-element.32), channel_id=1, source_target_pairs={{0,1},{1,2},{2,3},{3,4},{4,5},{5,6},{6,7},{7,0},{8,9},{9,10},{10,1... | collective-permute-start | bytes 3080 | tf_op jit(solution)/shard_map/ppermute | solution.py:17
  354.5 4.9 %collective-permute-start.58 = (f32[1,1,4,64]{3,2,1,0:T(4,128)S(1)}, f32[1,1,4,64]{3,2,1,0:T(4,128)S(1)}, u32[]{:S(2)}, u32[]{:S(2)}) collective-permute-start(f32[1,1,4,64]{3,2,1,0:T(4,128)S(1)} %get-tuple-element.33), channel_id=1, source_target_pairs={{1,0},{2,1},{3,2},{4,3},{5,4},{6,5},{7,6},{0,7},{9,8},{10,9},{11,1... | collective-permute-start | bytes 3080 | tf_op jit(solution)/shard_map/ppermute | solution.py:19
  369.4 6.0 %collective-permute-start.61 = (f32[2,4]{0,1:T(4,128)S(1)}, f32[2,4]{0,1:T(4,128)S(1)}, u32[]{:S(2)}, u32[]{:S(2)}) collective-permute-start(f32[2,4]{0,1:T(4,128)S(1)} %bitcast.210), channel_id=1, source_target_pairs={{0,7},{1,0},{2,1},{3,2},{4,3},{5,4},{6,5},{7,6},{8,15},{9,8},{10,9... | collective-permute-start | bytes 104 | tf_op jit(solution)/shard_map/ppermute | solution.py:61
  379.2 4.5 %collective-permute-start.63 = (f32[8,4]{0,1:T(4,128)S(1)}, f32[8,4]{0,1:T(4,128)S(1)}, u32[]{:S(2)}, u32[]{:S(2)}) collective-permute-start(f32[8,4]{0,1:T(4,128)S(1)} %pad_maximum_fusion.21), channel_id=1, source_target_pairs={{0,4},{1,5},{2,6},{3,7},{4,0},{5,1},{6,2},{7,3},{8,12},{9,13},{10,... | collective-permute-start | bytes 392 | tf_op jit(solution)/shard_map/ppermute | solution.py:61
  384.3 8.5 %collective-permute-start.66 = (f32[1,2,4,64]{3,2,1,0:T(4,128)S(1)}, f32[1,2,4,64]{3,2,1,0:T(4,128)S(1)}, u32[]{:S(2)}, u32[]{:S(2)}) collective-permute-start(f32[1,2,4,64]{3,2,1,0:T(4,128)S(1)} %get-tuple-element.26), channel_id=1, source_target_pairs={{0,8},{8,16},{16,24},{24,0},{1,9},{9,17},{17,25},{25,1},{2,10},{10... | collective-permute-start | bytes 6152 | tf_op jit(solution)/shard_map/ppermute | solution.py:17
  384.3 10.1 %collective-permute-start.67 = (f32[1,2,4,64]{3,2,1,0:T(4,128)S(1)}, f32[1,2,4,64]{3,2,1,0:T(4,128)S(1)}, u32[]{:S(2)}, u32[]{:S(2)}) collective-permute-start(f32[1,2,4,64]{3,2,1,0:T(4,128)S(1)} %get-tuple-element.26), channel_id=1, source_target_pairs={{8,0},{16,8},{24,16},{0,24},{9,1},{17,9},{25,17},{1,25},{10,2},{18... | collective-permute-start | bytes 6152 | tf_op jit(solution)/shard_map/ppermute | solution.py:19
  386.1 8.3 %collective-permute-start.64 = (f32[1,1,4,64]{3,2,1,0:T(4,128)S(1)}, f32[1,1,4,64]{3,2,1,0:T(4,128)S(1)}, u32[]{:S(2)}, u32[]{:S(2)}) collective-permute-start(f32[1,1,4,64]{3,2,1,0:T(4,128)S(1)} %get-tuple-element.28), channel_id=1, source_target_pairs={{0,1},{1,2},{2,3},{3,4},{4,5},{5,6},{6,7},{7,0},{8,9},{9,10},{10,1... | collective-permute-start | bytes 3080 | tf_op jit(solution)/shard_map/ppermute | solution.py:17
  389.4 5.1 %collective-permute-start.65 = (f32[1,1,4,64]{3,2,1,0:T(4,128)S(1)}, f32[1,1,4,64]{3,2,1,0:T(4,128)S(1)}, u32[]{:S(2)}, u32[]{:S(2)}) collective-permute-start(f32[1,1,4,64]{3,2,1,0:T(4,128)S(1)} %get-tuple-element.29), channel_id=1, source_target_pairs={{1,0},{2,1},{3,2},{4,3},{5,4},{6,5},{7,6},{0,7},{9,8},{10,9},{11,1... | collective-permute-start | bytes 3080 | tf_op jit(solution)/shard_map/ppermute | solution.py:19
  (10 other events, 71.0 us)
